TPU v7x, 32 devices: a whole 2x2x4 slice. The times are simulated.
32 devices in a mesh: grp: 2 (over y), ep: 16 (over z, x, core), sess: 1.
Axes of the slice: x: 2, y: 2, z: 4, core: 2. Of those that a mesh axis runs over, the one named last changes fastest.
Arguments:
- thinker_rows: bfloat16 [1024, 2048], P(('grp', 'ep', 'sess')), parts along dimension 0, may hold values from -6 to 6
- think_route: int32 [1024, 8], P(('grp', 'ep', 'sess')), parts along dimension 0, may hold values from 0 to 15, all different within a row; in each aligned block of 32 rows (0 to 31, 32 to 63, ...) at most 32 rows name the same one
- think_weight: float32 [1024, 8], P(('grp', 'ep', 'sess')), parts along dimension 0, may hold values from 0.1 to 1
- think_gate: bfloat16 [16, 2048, 768], P('ep', None, 'sess'), may hold values from -0.125 to 0.125
- think_up: bfloat16 [16, 2048, 768], P('ep', None, 'sess'), may hold values from -0.125 to 0.125
- think_down: bfloat16 [16, 768, 2048], P('ep', 'sess'), may hold values from -0.21875 to 0.21875
- proj_weight: bfloat16 [2048, 1024], P(None, 'sess'), may hold values from -0.125 to 0.125
- owner_map: int32 [1024], P(('grp', 'ep')), parts along dimension 0, may hold values from 0 to 31, as said below
- talk_gain: float32 [1024], replicated, may hold values from 0.5 to 1.5
- talk_route: int32 [1024, 6], P(('grp', 'ep', 'sess')), parts along dimension 0, may hold values from 0 to 15, all different within a row; in each aligned block of 32 rows (0 to 31, 32 to 63, ...) at most 24 rows name the same one
- talk_weight: float32 [1024, 6], P(('grp', 'ep', 'sess')), parts along dimension 0, may hold values from 0.1 to 1
- talk_gate: bfloat16 [16, 1024, 384], P(('ep', 'sess')), may hold values from -0.1875 to 0.1875
- talk_up: bfloat16 [16, 1024, 384], P(('ep', 'sess')), may hold values from -0.1875 to 0.1875
- talk_down: bfloat16 [16, 384, 1024], P(('ep', 'sess')), may hold values from -0.3125 to 0.3125
Outputs:
- thinker_branch: bfloat16 [1024, 2048], P(('grp', 'ep', 'sess')), parts along dimension 0
- talker_branch: bfloat16 [1024, 1024], P(('grp', 'ep', 'sess')), parts along dimension 0
There are 2 independent parts, one for each index of `grp`. A program takes and returns all parts, laid end to end along the dimension named above; an argument that names none is the same for every part. Nothing has to cross between parts.
Inputs may be any that keep to these rules, and one draw needn't show every extreme that they name: `think_route`: within each aligned block of 32 rows (the rows of one device) no thinker expert is named by more than 32 rows, a bound that some block reaches. `talk_route`: within each aligned block of 32 rows (the rows of one device) no talker expert is named by more than 24 rows, a bound that some block reaches. `owner_map`: each aligned block of 32 entries holds every value of its range exactly once.
All inputs are finite; a program needn't handle non-finite values.
Results may differ from a plain program's by a relative error of at most 0.015.
Values may be sent and summed in bfloat16 or wider, within the bound.
No kernel may reach another device: no remote copies, remote signals or barrier semaphores. Data moves between devices by JAX's collectives and lax.ppermute only.
A program may use at most 64 MiB of HBM per device.

v0:
```python
import jax
import jax.numpy as jnp
from jax import lax
from jax.sharding import PartitionSpec as P


def slot_places(route, experts):
    picks = route.shape[0] * route.shape[1]
    chosen = route.reshape(picks)
    onehot = (chosen[:, None] == jnp.arange(experts, dtype=jnp.int32)[None, :]).astype(jnp.int32)
    before = jnp.cumsum(onehot, axis=0) - onehot
    return (chosen, jnp.sum(before * onehot, axis=1))


def pack_rows(row_block, route, experts, capacity):
    chosen, places = slot_places(route, experts)
    target = chosen * capacity + places
    copies = jnp.repeat(row_block, route.shape[1], axis=0)
    buffer = (
        jnp.zeros((experts * capacity, row_block.shape[1]), jnp.bfloat16).at[target].set(copies)
    )
    return (buffer, target)


def combine_rows(returned, target, weights):
    sessions, picks = weights.shape
    gathered = returned[target].astype(jnp.float32).reshape(sessions, picks, returned.shape[1])
    norm_weights = weights / jnp.sum(weights, axis=1, keepdims=True)
    return jnp.sum(gathered * norm_weights[:, :, None], axis=1).astype(jnp.bfloat16)


def swiglu(slab, gate_m, up_m, down_m):
    gate = jnp.dot(slab, gate_m, preferred_element_type=jnp.float32)
    upper = jnp.dot(slab, up_m, preferred_element_type=jnp.float32)
    hidden = (jax.nn.silu(gate) * upper).astype(jnp.bfloat16)
    return jnp.dot(hidden, down_m, preferred_element_type=jnp.float32)


def on_device(
    thinker_rows,
    think_route,
    think_weight,
    think_gate,
    think_up,
    think_down,
    proj_weight,
    owner_map,
    talk_gain,
    talk_route,
    talk_weight,
    talk_gate,
    talk_up,
    talk_down,
):
    sessions = thinker_rows.shape[0]
    features = thinker_rows.shape[1]
    talk_features = talk_gate.shape[1]
    ep_count = lax.axis_size("ep")
    sess_count = lax.axis_size("sess")
    think_picks = think_route.shape[1]
    think_capacity = min(sessions, max(2, 2 * sessions * think_picks // ep_count))
    buffer, target = pack_rows(thinker_rows, think_route, ep_count, think_capacity)
    buffer = buffer.reshape(ep_count, think_capacity, features)
    gate_half = think_gate[0]
    up_half = think_up[0]
    down_half = think_down[0]
    paired = lax.all_gather(buffer, "sess", axis=1, tiled=True)
    arrived = lax.all_to_all(paired, "ep", split_axis=0, concat_axis=0, tiled=True)
    flattened = arrived.reshape(arrived.shape[0] * arrived.shape[1], features)
    result = swiglu(flattened, gate_half, up_half, down_half)
    partial_value = result.reshape(arrived.shape[0], arrived.shape[1], features)
    summed = lax.psum_scatter(partial_value, "sess", scatter_dimension=1, tiled=True).astype(
        jnp.bfloat16
    )
    returned = lax.all_to_all(summed, "ep", split_axis=0, concat_axis=0, tiled=True).reshape(
        ep_count * think_capacity, features
    )
    thinker_branch = combine_rows(returned, target, think_weight)
    projected = jnp.dot(
        lax.all_gather(thinker_branch, "sess", axis=0, tiled=True),
        proj_weight,
        preferred_element_type=jnp.float32,
    ).astype(jnp.bfloat16)
    block_rows = owner_map.shape[0]
    picker = (owner_map[:, None] == jnp.arange(block_rows, dtype=jnp.int32)[None, :]).astype(
        jnp.bfloat16
    )
    selected = jnp.dot(picker, projected, preferred_element_type=jnp.float32).astype(jnp.bfloat16)
    own_rows = lax.all_to_all(selected, "sess", split_axis=0, concat_axis=1, tiled=True).astype(
        jnp.float32
    )
    scale = lax.rsqrt(jnp.mean(own_rows * own_rows, axis=1, keepdims=True) + 1e-06)
    talk_rows = (own_rows * scale * talk_gain[None, :]).astype(jnp.bfloat16)
    talk_experts = ep_count * sess_count
    talk_picks = talk_route.shape[1]
    talk_capacity = min(sessions, max(2, 2 * sessions * talk_picks // talk_experts))
    talk_buffer, talk_target = pack_rows(talk_rows, talk_route, talk_experts, talk_capacity)
    talk_gate_m = talk_gate[0]
    talk_up_m = talk_up[0]
    talk_down_m = talk_down[0]
    sectioned_in = talk_buffer.reshape(talk_experts, talk_capacity, talk_features)
    portion = lax.all_to_all(sectioned_in, ("ep", "sess"), split_axis=0, concat_axis=0, tiled=True)
    flattened = portion.reshape(portion.shape[0] * portion.shape[1], talk_features)
    result = swiglu(flattened, talk_gate_m, talk_up_m, talk_down_m).astype(jnp.bfloat16)
    finished = result.reshape(portion.shape[0], portion.shape[1], talk_features)
    talk_returned = lax.all_to_all(
        finished, ("ep", "sess"), split_axis=0, concat_axis=0, tiled=True
    )
    talk_returned = talk_returned.reshape(talk_experts * talk_capacity, talk_features)
    talker_branch = combine_rows(talk_returned, talk_target, talk_weight)
    return (thinker_branch, talker_branch)


def solution(mesh):
    return jax.shard_map(
        on_device,
        mesh=mesh,
        in_specs=(
            P(("grp", "ep", "sess"), None),
            P(("grp", "ep", "sess"), None),
            P(("grp", "ep", "sess"), None),
            P("ep", None, "sess"),
            P("ep", None, "sess"),
            P("ep", "sess", None),
            P(None, "sess"),
            P(("grp", "ep")),
            P(),
            P(("grp", "ep", "sess"), None),
            P(("grp", "ep", "sess"), None),
            P(("ep", "sess"), None, None),
            P(("ep", "sess"), None, None),
            P(("ep", "sess"), None, None),
        ),
        out_specs=(P(("grp", "ep", "sess"), None), P(("grp", "ep", "sess"), None)),
        check_vma=False,
    )
```

profile of v0, /device:TPU:0, one launch (start us, length us, event | category | flops | bytes accessed | tf_op | source)
XLA Modules:
  0.0 198.5 jit_solution(11233426800232921095)
XLA Ops:
  0.6 0.0 copy-start
  0.6 0.9 copy.19
  1.6 0.1 eq.64
  1.6 0.1 eq.60
  1.7 0.7 broadcast_multiply_fusion.1
  2.4 0.6 reduce-window.14
  3.0 0.2 slice_reduce_fusion.1
  3.2 0.1 copy.18
  3.3 0.1 mul.89
  3.4 0.1 fusion.33
  3.5 4.1 %scatter_custom_fusion = bf16[512,2048]{1,0:T(8,128)(2,1)} fusion(s32[256]{0:T(256)S(1)} %bitcast.89, bf16[]{:T(256)} %constant.11.clone.1, bf16[32,2048]{1,0:T(8,128)(2,1)} %param.14), kind=kCustom, calls=%fused_computation.20 | custom fusion | bytes 2228226 | tf_op jit(solution)/shard_map/scatter | solution.py:20
  7.6 0.0 copy-start.10
  7.6 54.8 %all_to_all.20 = bf16[16,32,2048]{2,1,0:T(8,128)(2,1)S(1)} all-to-all(bf16[16,32,2048]{2,1,0:T(8,128)(2,1)} %bitcast.80), channel_id=1, replica_groups=mesh['grp'=2,'ep'=16,'sess'=1] {'ep'}, dimensions={0} | all-to-all | bytes 4194304 | tf_op jit(solution)/shard_map/all_to_all | solution.py:68
  62.4 0.0 copy-done.10
  62.4 0.0 copy-start.11
  62.4 1.8 fusion.4
  64.3 0.1 copy-done.11
  64.3 1.9 multiply_convert_fusion
  66.2 0.0 copy-done
  66.2 3.1 %fusion.6 = bf16[16,32,2048]{2,1,0:T(8,128)(2,1)} fusion(bf16[16,32,768]{2,1,0:T(8,128)(2,1)S(1)} %bitcast.93, bf16[1,768,2048]{2,1,0:T(8,128)(2,1)S(1)} %copy-done), kind=kOutput, calls=%fused_computation.10 | convolution fusion | flops 1611661312 | bytes 6029312 | tf_op jit(solution)/shard_map/dot_general | solution.py:36
  69.4 0.0 copy-start.4
  69.4 0.0 copy-start.3
  69.4 5.3 %all-to-all-start.1 = ((bf16[16,32,2048]{2,1,0:T(8,128)(2,1)}), bf16[16,32,2048]{2,1,0:T(8,128)(2,1)}, u32[]{:S(2)}, u32[]{:S(2)}) async-start(bf16[16,32,2048]{2,1,0:T(8,128)(2,1)} %fusion.6), calls=%async_computation.1 | async-start | bytes 4194304 | tf_op jit(solution)/shard_map/all_to_all | solution.py:75
  74.7 0.0 copy-done.4
  74.8 0.1 copy.22
  74.8 0.0 copy-done.3
  74.8 0.1 copy.24
  74.9 0.1 eq.68
  75.1 0.6 reduce-window.16
  75.7 0.2 slice_reduce_fusion
  75.9 0.1 copy.23
  76.0 0.1 mul.97
  76.1 0.1 bitcast_bitcast_fusion
  76.2 0.0 copy-start.7
  76.2 39.5 %all-to-all-done.1 = bf16[16,32,2048]{2,1,0:T(8,128)(2,1)} async-done(((bf16[16,32,2048]{2,1,0:T(8,128)(2,1)}), bf16[16,32,2048]{2,1,0:T(8,128)(2,1)}, u32[]{:S(2)}, u32[]{:S(2)}) %all-to-all-start.1) | async-done | bytes 2097184 | tf_op jit(solution)/shard_map/all_to_all | solution.py:75
  115.7 0.0 copy-start.9
  115.7 5.2 %gather_fusion = bf16[256,2048]{1,0:T(8,128)(2,1)} fusion(bf16[512,2048]{1,0:T(8,128)(2,1)} %bitcast.11, s32[1024]{0:T(1024)S(1)} %pad_clamp_fusion.1), kind=kCustom, calls=%fused_computation | custom fusion | bytes 2098176 | tf_op jit(solution)/shard_map/gather | solution.py:27
  121.0 2.2 %fusion.9 = bf16[32,2048]{1,0:T(8,128)(2,1)S(1)} fusion(bf16[256,2048]{1,0:T(8,128)(2,1)} %gather_fusion, f32[32,8]{1,0:T(8,128)S(1)} %copy.22), kind=kLoop, calls=%fused_computation.12 | loop fusion | flops 1507328 | bytes 1180672 | tf_op jit(solution)/shard_map/reduce_sum | solution.py:29
  123.2 0.0 copy-done.9
  123.2 0.0 copy-start.2
  123.2 0.0 copy-start.6
  123.2 3.3 %multiply_reduce_fusion.1 = (f32[32]{0:T(128)S(1)}, f32[32,1024]{1,0:T(8,128)S(1)}) fusion(bf16[32,2048]{1,0:T(8,128)(2,1)S(1)} %fusion.9, bf16[2048,1024]{1,0:T(8,128)(2,1)} %param.20, s32[32]{0:T(128)S(1)} %copy-done.9), kind=kOutput, calls=%fused_computation.38 | convolution fusion | flops 136479712 | bytes 4456704 | tf_op jit(solution)/shard_map/dot_general | solution.py:88
  126.5 0.0 copy-done.2
  126.5 0.0 copy-done.6
  126.6 0.1 multiply_convert_fusion.1
  126.6 0.9 broadcast_in_dim.11
  127.5 1.2 reshape.185
  128.7 0.0 copy-done.7
  128.7 2.3 %scatter_custom_fusion.1 = bf16[384,1024]{1,0:T(8,128)(2,1)} fusion(s32[192]{0:T(256)S(1)} %bitcast.87, bf16[192,1024]{1,0:T(8,128)(2,1)S(1)} %reshape.185, bf16[]{:T(256)} %constant.11.clone.1), kind=kCustom, calls=%fused_computation.34 | custom fusion | bytes 786434 | tf_op jit(solution)/shard_map/scatter | solution.py:20
  131.0 31.3 %all_to_all.21 = bf16[16,24,1024]{2,1,0:T(8,128)(2,1)S(1)} all-to-all(bf16[16,24,1024]{2,1,0:T(8,128)(2,1)} %bitcast.81), channel_id=1, replica_groups=mesh['grp'=2,'ep'=16,'sess'=1] {'ep','sess'}, dimensions={0} | all-to-all | bytes 1572864 | tf_op jit(solution)/shard_map/all_to_all | solution.py:102
  162.4 0.9 copy-done.1
  163.3 2.5 %fusion.20 = f32[384,384]{1,0:T(8,128)} fusion(bf16[384,1024]{1,0:T(8,128)(2,1)S(1)} %bitcast.82, bf16[1,1024,384]{2,1,0:T(8,128)(2,1)} %param.25), kind=kOutput, calls=%fused_computation.26 | convolution fusion | flops 301989888 | bytes 2162688 | tf_op jit(solution)/shard_map/dot_general | solution.py:33
  165.8 0.0 copy-start.5
  165.8 0.0 copy-start.8
  165.8 3.7 %convolution_convert_fusion = bf16[384,1024]{1,0:T(8,128)(2,1)} fusion(bf16[384,1024]{1,0:T(8,128)(2,1)} %bitcast.83, bf16[1,384,1024]{2,1,0:T(8,128)(2,1)} %param.27, bf16[1,1024,384]{2,1,0:T(8,128)(2,1)} %param.26, f32[384,384]{1,0:T(8,128)} %fusion.20), kind=kOutput, calls=%fused_computation.14 | convolution fusion | flops 605257728 | bytes 3735552 | tf_op jit(solution)/shard_map/dot_general | solution.py:36
  169.5 4.3 %all-to-all-start.3 = ((bf16[16,24,1024]{2,1,0:T(8,128)(2,1)}), bf16[16,24,1024]{2,1,0:T(8,128)(2,1)}, u32[]{:S(2)}, u32[]{:S(2)}) async-start(bf16[16,24,1024]{2,1,0:T(8,128)(2,1)} %bitcast.86), calls=%async_computation.3 | async-start | bytes 1572864 | tf_op jit(solution)/shard_map/all_to_all | solution.py:106
  173.8 0.0 copy-done.5
  173.9 0.1 copy.27
  174.0 0.0 copy-done.8
  174.0 0.6 pad_clamp_fusion
  174.6 18.0 %all-to-all-done.3 = bf16[16,24,1024]{2,1,0:T(8,128)(2,1)} async-done(((bf16[16,24,1024]{2,1,0:T(8,128)(2,1)}), bf16[16,24,1024]{2,1,0:T(8,128)(2,1)}, u32[]{:S(2)}, u32[]{:S(2)}) %all-to-all-start.3) | async-done | bytes 786464 | tf_op jit(solution)/shard_map/all_to_all | solution.py:106
  192.5 2.7 %gather_fusion.1 = bf16[192,1024]{1,0:T(8,128)(2,1)S(1)} fusion(bf16[384,1024]{1,0:T(8,128)(2,1)} %bitcast.22, s32[1024]{0:T(1024)} %pad_clamp_fusion), kind=kCustom, calls=%fused_computation.1 | custom fusion | bytes 787200 | tf_op jit(solution)/shard_map/gather | solution.py:27
  195.2 1.1 reshape.156
  196.3 2.3 %multiply_reduce_fusion = bf16[32,1024]{1,0:T(8,128)(2,1)} fusion(f32[32,6,1024]{2,1,0:T(8,128)} %reshape.156, f32[32,6]{1,0:T(8,128)S(1)} %copy.27), kind=kLoop, calls=%fused_computation.22 | loop fusion | flops 360448 | bytes 852736 | tf_op jit(solution)/shard_map/reduce_sum | solution.py:29
  (18 shorter events, 0.2 us)
Async XLA Ops:
  0.6 65.6 %copy-start = (bf16[1,768,2048]{2,1,0:T(8,128)(2,1)S(1)}, bf16[1,768,2048]{2,1,0:T(8,128)(2,1)}, u32[]{:S(2)}) copy-start(bf16[1,768,2048]{2,1,0:T(8,128)(2,1)} %param.19) | copy-start | bytes 9437188
  7.6 54.8 %copy-start.10 = (bf16[1,2048,768]{2,1,0:T(8,128)(2,1)S(1)}, bf16[1,2048,768]{2,1,0:T(8,128)(2,1)}, u32[]{:S(2)}) copy-start(bf16[1,2048,768]{2,1,0:T(8,128)(2,1)} %param.17) | copy-start | bytes 9437188
  62.4 1.9 copy-start.11
  69.4 5.4 %copy-start.4 = (f32[32,8]{0,1:T(8,128)S(1)}, f32[32,8]{0,1:T(8,128)}, u32[]{:S(2)}) copy-start(f32[32,8]{0,1:T(8,128)} %param.16) | copy-start | bytes 3076
  69.4 5.5 %copy-start.3 = (s32[32,6]{0,1:T(8,128)S(1)}, s32[32,6]{0,1:T(8,128)}, u32[]{:S(2)}) copy-start(s32[32,6]{0,1:T(8,128)} %param.23) | copy-start | bytes 2308
  69.4 46.4 %all-to-all-start.1 = ((bf16[16,32,2048]{2,1,0:T(8,128)(2,1)}), bf16[16,32,2048]{2,1,0:T(8,128)(2,1)}, u32[]{:S(2)}, u32[]{:S(2)}) async-start(bf16[16,32,2048]{2,1,0:T(8,128)(2,1)} %fusion.6), calls=%async_computation.1 | async-start | bytes 4194304 | tf_op jit(solution)/shard_map/all_to_all | solution.py:75
  76.2 52.5 %copy-start.7 = (s32[192,1]{0,1:T(1,128)}, s32[192,1]{0,1:T(1,128)S(1)}, u32[]{:S(2)}) copy-start(s32[192,1]{0,1:T(1,128)S(1)} %compare_select_fusion) | copy-start | bytes 2308
  115.7 7.4 %copy-start.9 = (s32[32]{0:T(128)S(1)}, s32[32]{0:T(128)}, u32[]{:S(2)}) copy-start(s32[32]{0:T(128)} %param.21) | copy-start | bytes 388
  123.2 3.3 %copy-start.2 = (bf16[32,2048]{1,0:T(8,128)(2,1)}, bf16[32,2048]{1,0:T(8,128)(2,1)S(1)}, u32[]{:S(2)}) copy-start(bf16[32,2048]{1,0:T(8,128)(2,1)S(1)} %fusion.9) | copy-start | bytes 393220
  123.2 3.3 %copy-start.6 = (f32[1024]{0:T(1024)S(1)}, f32[1024]{0:T(1024)}, u32[]{:S(2)}) copy-start(f32[1024]{0:T(1024)} %param.22) | copy-start | bytes 12292
  162.4 0.9 copy-start.1
  165.8 8.0 %copy-start.5 = (f32[32,6]{0,1:T(8,128)S(1)}, f32[32,6]{0,1:T(8,128)}, u32[]{:S(2)}) copy-start(f32[32,6]{0,1:T(8,128)} %param.24) | copy-start | bytes 2308
  165.8 8.1 %copy-start.8 = (s32[192,1]{0,1:T(1,128)S(1)}, s32[192,1]{0,1:T(1,128)}, u32[]{:S(2)}) copy-start(s32[192,1]{0,1:T(1,128)} %copy-done.7) | copy-start | bytes 2308
  169.5 23.0 %all-to-all-start.3 = ((bf16[16,24,1024]{2,1,0:T(8,128)(2,1)}), bf16[16,24,1024]{2,1,0:T(8,128)(2,1)}, u32[]{:S(2)}, u32[]{:S(2)}) async-start(bf16[16,24,1024]{2,1,0:T(8,128)(2,1)} %bitcast.86), calls=%async_computation.3 | async-start | bytes 1572864 | tf_op jit(solution)/shard_map/all_to_all | solution.py:106
where the time goes:
time: 199 us
  blocking collectives  86.1 us (43%)
  waiting for transfers between devices  57.5 us (29%)
  local copies, waits for them, and re-layouts  20.7 us (10%)
  matrix products  16.4 us (8%)
  starting transfers between devices  9.62 us (5%)
  other arithmetic  7.37 us (4%)
    all_to_all x1, blocking collectives, on_device(): lax.all_to_all(paired, 'ep', split_axis=0, concat_axis=0, tiled=True)  54.8 us
    all_to_all x1, waiting for transfers between devices, on_device(): lax.all_to_all(summed, 'ep', split_axis=0, concat_axis=0, tiled=True)  39.5 us
    all_to_all x1, blocking collectives, on_device(): lax.all_to_all(sectioned_in, ('ep', 'sess'), split_axis=0, concat_axis=0,...  31.3 us
    all_to_all x1, waiting for transfers between devices, on_device(): lax.all_to_all(finished, ('ep', 'sess'), split_axis=0, concat_axis=0, til...  18 us
    gather x2, local copies, waits for them, and re-layouts, combine_rows(): returned[target].astype(jnp.float32)  7.89 us
    dot_general x2, matrix products, swiglu(): return jnp.dot(hidden, down_m, preferred_element_type=jnp.float32)  6.85 us
    scatter x2, local copies, waits for them, and re-layouts, pack_rows(): jnp.zeros((experts * capacity, row_block.shape[1]), jnp.bfloat16).at[target]  6.46 us
    all_to_all x1, starting transfers between devices, on_device(): lax.all_to_all(summed, 'ep', split_axis=0, concat_axis=0, tiled=True)  5.34 us
  transfers between devices with their start and end apart: 2, of which 2 were waited for; matrix products, arithmetic and copies ran while one was open for 1% of the time, Pallas kernels for 0%

commit v1 on v0

--- a/solution.py
+++ b/solution.py
@@ -1,6 +1,10 @@
+import functools
+
 import jax
 import jax.numpy as jnp
 from jax import lax
+from jax.experimental import pallas as pl
+from jax.experimental.pallas import tpu as pltpu
 from jax.sharding import PartitionSpec as P
 
 
@@ -111,9 +115,253 @@
     return (thinker_branch, talker_branch)
 
 
+VMEM = pl.BlockSpec(memory_space=pltpu.VMEM)
+SMEM = pl.BlockSpec(memory_space=pltpu.SMEM)
+LANES = 128
+
+
+def width_of_table(experts):
+    return -(-4 * experts // LANES) * LANES
+
+
+def share_table(lane, route_ref, weight_ref, first, experts):
+    weights = weight_ref[...]
+    shares = weights / jnp.sum(weights, axis=1, keepdims=True)
+    table = jnp.zeros(lane.shape, jnp.float32)
+    for pick in range(weights.shape[1]):
+        expert = route_ref[:, pick : pick + 1] + first
+        hit = (lane == expert) | (lane == expert + experts)
+        table = table + jnp.where(hit, shares[:, pick : pick + 1], 0.0)
+    return table
+
+
+def pack_kernel(experts, rows_ref, route_ref, weight_ref, talk_route_ref, talk_weight_ref, out_ref):
+    count, features = rows_ref.shape
+    out_ref[:, :features] = rows_ref[...]
+    lane = lax.broadcasted_iota(jnp.int32, (count, out_ref.shape[1] - features), 1)
+    table = share_table(lane, route_ref, weight_ref, 0, experts)
+    table = table + share_table(lane, talk_route_ref, talk_weight_ref, 2 * experts, experts)
+    high = table.astype(jnp.bfloat16).astype(jnp.float32)
+    fine = ((lane >= experts) & (lane < 2 * experts)) | (lane >= 3 * experts)
+    out_ref[:, features:] = jnp.where(fine, table - high, high).astype(jnp.bfloat16)
+
+
+def pack(rows, route, weight, talk_route, talk_weight, experts):
+    count, features = rows.shape
+    return pl.pallas_call(
+        functools.partial(pack_kernel, experts),
+        out_shape=jax.ShapeDtypeStruct((count, features + width_of_table(experts)), jnp.bfloat16),
+        in_specs=[VMEM] * 5,
+        out_specs=VMEM,
+        compiler_params=pltpu.CompilerParams(vmem_limit_bytes=8 << 20),
+        cost_estimate=pl.CostEstimate(flops=1 << 20, bytes_accessed=1 << 18, transcendentals=0),
+        name="pack",
+    )(rows, route, weight, talk_route, talk_weight)
+
+
+def share_of(columns, first, experts, expert):
+    lane = lax.broadcasted_iota(jnp.int32, columns.shape, 1)
+    hit = (lane == first + expert) | (lane == first + experts + expert)
+    return jnp.sum(jnp.where(hit, columns.astype(jnp.float32), 0.0), axis=1, keepdims=True)
+
+
+def tile_of(width, most):
+    tile = min(width, most)
+    while width % tile:
+        tile -= LANES
+    return tile
+
+
+def experts_of_block(slab_ref, hidden_ref, share, gate_ref, up_ref, down_ref, put):
+    slab = slab_ref[...]
+    hidden_units = gate_ref.shape[-1]
+    step = tile_of(hidden_units, 256)
+    for start in range(0, hidden_units, step):
+        cut = slice(start, start + step)
+        gate = jnp.dot(slab, gate_ref[0, :, cut], preferred_element_type=jnp.float32)
+        upper = jnp.dot(slab, up_ref[0, :, cut], preferred_element_type=jnp.float32)
+        hidden = gate / (1.0 + jnp.exp(-gate)) * upper
+        hidden_ref[:, cut] = (hidden * share).astype(jnp.bfloat16)
+    hidden = hidden_ref[...]
+    features = down_ref.shape[-1]
+    step = tile_of(features, 512)
+    for start in range(0, features, step):
+        cut = slice(start, start + step)
+        put(cut, jnp.dot(hidden, down_ref[0, :, cut], preferred_element_type=jnp.float32))
+
+
+def expert_kernel(count, groups, experts, first, expert_ref, *refs):
+    blocks = refs[:count]
+    tables = refs[count : 2 * count]
+    gate_ref, up_ref, down_ref = refs[2 * count : 2 * count + 3]
+    outs = refs[2 * count + 3 : -2]
+    slab_ref, hidden_ref = refs[-2:]
+    rows = blocks[0].shape[0]
+    features = slab_ref.shape[1]
+    shares = []
+    for index, (block, table) in enumerate(zip(blocks, tables, strict=True)):
+        slab_ref[index * rows : (index + 1) * rows, :] = block[:, :features]
+        columns = table[:, table.shape[1] - width_of_table(experts) :]
+        shares.append(share_of(columns, first, experts, expert_ref[0]))
+    share = jnp.concatenate(shares, axis=0)
+
+    def put(cut, value):
+        value = value.astype(jnp.bfloat16)
+        for out, group in zip(outs, groups, strict=True):
+            for place, index in enumerate(group):
+                out[place * rows : (place + 1) * rows, cut] = value[index * rows : (index + 1) * rows]
+
+    experts_of_block(slab_ref, hidden_ref, share, gate_ref, up_ref, down_ref, put)
+
+
+def run_expert(blocks, tables, groups, gate, up, down, expert, experts, first, name):
+    count, rows = len(blocks), blocks[0].shape[0]
+    _, features, hidden_units = gate.shape
+    total = count * rows
+    limit = 4 * total * features + 4 * total * hidden_units + (16 << 20)
+    return pl.pallas_call(
+        functools.partial(expert_kernel, count, groups, experts, first),
+        out_shape=[jax.ShapeDtypeStruct((len(g) * rows, features), jnp.bfloat16) for g in groups],
+        in_specs=[SMEM] + [VMEM] * (2 * count + 3),
+        out_specs=[VMEM] * len(groups),
+        scratch_shapes=[
+            pltpu.VMEM((total, features), jnp.bfloat16),
+            pltpu.VMEM((total, hidden_units), jnp.bfloat16),
+        ],
+        compiler_params=pltpu.CompilerParams(vmem_limit_bytes=limit),
+        cost_estimate=pl.CostEstimate(
+            flops=6 * total * features * hidden_units,
+            bytes_accessed=6 * features * hidden_units,
+            transcendentals=total * hidden_units,
+        ),
+        name=name,
+    )(expert, *blocks, *tables, gate, up, down)
+
+
+def relay_kernel(count, *refs):
+    parts = refs[:count]
+    proj_ref, owner_ref, gain_ref, branch_ref, rows_ref = refs[count:]
+    rows = branch_ref.shape[0]
+    total = parts[0][...].astype(jnp.float32)[:rows]
+    for part in parts[1:]:
+        total = total + part[...].astype(jnp.float32)[:rows]
+    branch = total.astype(jnp.bfloat16)
+    branch_ref[...] = branch
+    source = lax.broadcasted_iota(jnp.int32, (rows, rows), 1)
+    picker = (owner_ref[...] == source).astype(jnp.bfloat16)
+    chosen = jnp.dot(picker, branch, preferred_element_type=jnp.float32).astype(jnp.bfloat16)
+    relayed = jnp.dot(chosen, proj_ref[...], preferred_element_type=jnp.float32)
+    relayed = relayed.astype(jnp.bfloat16).astype(jnp.float32)
+    scale = lax.rsqrt(jnp.mean(relayed * relayed, axis=1, keepdims=True) + 1e-06)
+    rows_ref[...] = (relayed * scale * gain_ref[...]).astype(jnp.bfloat16)
+
+
+def relay(parts, proj, owner, gain):
+    rows = owner.shape[0]
+    features, talk_features = proj.shape
+    return pl.pallas_call(
+        functools.partial(relay_kernel, len(parts)),
+        out_shape=[
+            jax.ShapeDtypeStruct((rows, features), jnp.bfloat16),
+            jax.ShapeDtypeStruct((rows, talk_features), jnp.bfloat16),
+        ],
+        in_specs=[VMEM] * (len(parts) + 3),
+        out_specs=[VMEM] * 2,
+        compiler_params=pltpu.CompilerParams(vmem_limit_bytes=16 << 20),
+        cost_estimate=pl.CostEstimate(
+            flops=2 * rows * features * talk_features,
+            bytes_accessed=2 * features * talk_features,
+            transcendentals=0,
+        ),
+        name="relay",
+    )(*parts, proj, owner[:, None], gain[None, :])
+
+
+def swap(value, bit, count):
+    return lax.ppermute(value, "ep", [(i, i ^ bit) for i in range(count)])
+
+
+def gather_blocks(own, count):
+    blocks = {0: own}
+    bit = count // 2
+    while bit:
+        for mask in sorted(blocks):
+            blocks[mask | bit] = swap(blocks[mask], bit, count)
+        bit //= 2
+    return blocks
+
+
+def add_up(*terms):
+    total = terms[0].astype(jnp.float32)
+    for term in terms[1:]:
+        total = total + term.astype(jnp.float32)
+    return total.astype(jnp.bfloat16)
+
+
+def scatter_sums(blocks, count):
+    parts = {mask: [block] for mask, block in blocks.items()}
+    bit = 1
+    while bit < count:
+        for mask in sorted((m for m in parts if m & bit), reverse=True):
+            sent = parts.pop(mask)
+            parts[mask ^ bit].append(swap(sent[0] if len(sent) == 1 else add_up(*sent), bit, count))
+        bit *= 2
+    return parts[0]
+
+
+def by_gathering(
+    thinker_rows,
+    think_route,
+    think_weight,
+    think_gate,
+    think_up,
+    think_down,
+    proj_weight,
+    owner_map,
+    talk_gain,
+    talk_route,
+    talk_weight,
+    talk_gate,
+    talk_up,
+    talk_down,
+):
+    count = lax.axis_size("ep")
+    expert = lax.axis_index("ep").astype(jnp.int32).reshape(1)
+    packed = pack(thinker_rows, think_route, think_weight, talk_route, talk_weight, count)
+    gathered = gather_blocks(packed, count)
+    done = {}
+    for half in range(2):
+        masks = list(range(half * count // 2, (half + 1) * count // 2))
+        blocks = [gathered[m] for m in masks]
+        groups = [[i] for i in range(len(masks))]
+        outs = run_expert(
+            blocks, blocks, groups, think_gate, think_up, think_down, expert, count, 0, "thinker"
+        )
+        done.update(zip(masks, outs, strict=True))
+    thinker_branch, talk_rows = relay(scatter_sums(done, count), proj_weight, owner_map, talk_gain)
+    talk_blocks = gather_blocks(talk_rows, count)
+    masks = list(range(count))
+    outs = run_expert(
+        [talk_blocks[m] for m in masks],
+        [gathered[m][:, thinker_rows.shape[1] :] for m in masks],
+        [[i] for i in masks],
+        talk_gate,
+        talk_up,
+        talk_down,
+        expert,
+        count,
+        2 * count,
+        "talker",
+    )
+    talker_branch = add_up(*scatter_sums(dict(zip(masks, outs, strict=True)), count))
+    return (thinker_branch, talker_branch)
+
+
 def solution(mesh):
+    count = mesh.shape["ep"]
+    dense = mesh.shape["sess"] == 1 and count & (count - 1) == 0 and count <= 16
     return jax.shard_map(
-        on_device,
+        by_gathering if dense else on_device,
         mesh=mesh,
         in_specs=(
             P(("grp", "ep", "sess"), None),

time: 199 us -> 107 us (0.54)
  blocking collectives: 86.1 us -> 0 us
  starting transfers between devices: 9.62 us -> 43.9 us
  waiting for transfers between devices: 57.5 us -> 38.6 us
  matrix products: 16.4 us -> 0 us
  Pallas kernels: 0 us -> 9.75 us
  local copies, waits for them, and re-layouts: 20.7 us -> 12 us
  other arithmetic: 7.37 us -> 1.15 us
    all_to_all x2 -> x0, blocking collectives: 86.1 us -> none  [the longest x1 54.8 us: on_device(): lax.all_to_all(paired, 'ep', split_axis=0, concat_axis=0, tiled=True)]
    all_to_all x2 -> x0, waiting for transfers between devices: 57.5 us -> none  [the longest x1 39.5 us: on_device(): lax.all_to_all(summed, 'ep', split_axis=0, concat_axis=0, tiled=True)]
    ppermute x0 -> x60, starting transfers between devices: none -> 43.9 us  [swap(): return lax.ppermute(value, 'ep', [(i, i ^ bit) for i in range(count)])]
    ppermute x0 -> x60, waiting for transfers between devices: none -> 38.6 us  [swap(): return lax.ppermute(value, 'ep', [(i, i ^ bit) for i in range(count)])]
    dot_general x6 -> x0, matrix products: 16.4 us -> none  [the longest x2 6.85 us: swiglu(): return jnp.dot(hidden, down_m, preferred_element_type=jnp.float32)]
    unnamed x26 -> x30, local copies, waits for them, and re-layouts: 2.03 us -> 11.8 us
    pallas_call x0 -> x5, Pallas kernels: none -> 9.75 us  [the longest x3 7.82 us: run_expert(): pl.pallas_call(functools.partial(expert_kernel, count, groups, experts, f...]
    all_to_all x2 -> x0, starting transfers between devices: 9.62 us -> none  [the longest x1 5.34 us: on_device(): lax.all_to_all(summed, 'ep', split_axis=0, concat_axis=0, tiled=True)]
  transfers between devices with their start and end apart: 2 -> 60, of which waited for: 2 -> 25; matrix products, arithmetic and copies ran while one was open for 1% -> 1% of each run, Pallas kernels for 0% -> 5%
where the time goes in v1:
time: 107 us; the launch traced here: 106 us
  starting transfers between devices  43.9 us (41%)
  waiting for transfers between devices  38.6 us (36%)
  local copies, waits for them, and re-layouts  12 us (11%)
  Pallas kernels  9.75 us (9%)
  other arithmetic  1.15 us (1%)
    ppermute x60, starting transfers between devices, swap(): return lax.ppermute(value, 'ep', [(i, i ^ bit) for i in range(count)])  43.9 us
    ppermute x60, waiting for transfers between devices, swap(): return lax.ppermute(value, 'ep', [(i, i ^ bit) for i in range(count)])  38.6 us
    unnamed x30, local copies, waits for them, and re-layouts  11.8 us
    pallas_call x3, Pallas kernels, run_expert(): pl.pallas_call(functools.partial(expert_kernel, count, groups, experts, f...  7.82 us
  transfers between devices with their start and end apart: 60, of which 25 were waited for; matrix products, arithmetic and copies ran while one was open for 1% of the time, Pallas kernels for 5%

profile of v1, /device:TPU:0, one launch (start us, length us, event | category | flops | bytes accessed | tf_op | source)
XLA Modules:
  0.0 106.5 jit_solution(7792283490816886007)
XLA Ops:
  0.6 0.8 copy.16.route_ref
  1.4 0.8 copy.17.weight_ref
  2.2 0.8 copy.18.talk_route_ref
  2.9 0.8 copy.19.talk_weight_ref
  3.7 0.9 copy-done.7
  5.0 3.1 %collective-permute-start.3 = (bf16[32,2176]{1,0:T(8,128)(2,1)S(1)}, bf16[32,2176]{1,0:T(8,128)(2,1)S(1)}, u32[]{:S(2)}, u32[]{:S(2)}) collective-permute-start(bf16[32,2176]{1,0:T(8,128)(2,1)S(1)} %pack.1.refs_0_.refs_8_), channel_id=1, source_target_pairs={{0,4},{1,5},{2,6},{3,7},{4,0},{5,1},{6,2},{7,3},{8,12},{9,13},{10,... | collective-permute-start | bytes 417800 | tf_op jit(solution)/shard_map/ppermute | solution.py:281
  8.1 2.6 %collective-permute-start.14 = (bf16[32,2176]{1,0:T(8,128)(2,1)S(1)}, bf16[32,2176]{1,0:T(8,128)(2,1)S(1)}, u32[]{:S(2)}, u32[]{:S(2)}) collective-permute-start(bf16[32,2176]{1,0:T(8,128)(2,1)S(1)} %pack.1.refs_0_.refs_8_), channel_id=1, source_target_pairs={{0,8},{1,9},{2,10},{3,11},{4,12},{5,13},{6,14},{7,15},{8,0},{9,1},... | collective-permute-start | bytes 417800 | tf_op jit(solution)/shard_map/ppermute | solution.py:281
  10.7 1.5 %collective-permute-start.1 = (bf16[32,2176]{1,0:T(8,128)(2,1)S(1)}, bf16[32,2176]{1,0:T(8,128)(2,1)S(1)}, u32[]{:S(2)}, u32[]{:S(2)}) collective-permute-start(bf16[32,2176]{1,0:T(8,128)(2,1)S(1)} %pack.1.refs_0_.refs_8_), channel_id=1, source_target_pairs={{0,2},{1,3},{2,0},{3,1},{4,6},{5,7},{6,4},{7,5},{8,10},{9,11},{10,... | collective-permute-start | bytes 417800 | tf_op jit(solution)/shard_map/ppermute | solution.py:281
  12.2 1.8 %collective-permute-done.3.refs_4_.refs_12_ = bf16[32,2176]{1,0:T(8,128)(2,1)S(1)} collective-permute-done((bf16[32,2176]{1,0:T(8,128)(2,1)S(1)}, bf16[32,2176]{1,0:T(8,128)(2,1)S(1)}, u32[]{:S(2)}, u32[]{:S(2)}) %collective-permute-start.3) | collective-permute-done | bytes 139296 | tf_op jit(solution)/shard_map/ppermute | solution.py:281
  14.0 1.8 %collective-permute-start.5 = (bf16[32,2176]{1,0:T(8,128)(2,1)S(1)}, bf16[32,2176]{1,0:T(8,128)(2,1)S(1)}, u32[]{:S(2)}, u32[]{:S(2)}) collective-permute-start(bf16[32,2176]{1,0:T(8,128)(2,1)S(1)} %collective-permute-done.3.refs_4_.refs_12_), channel_id=1, source_target_pairs={{0,2},{1,3},{2,0},{3,1},{4,6},{5,7},{6,4},{7,5},{8,10},{9,11},{10,... | collective-permute-start | bytes 417800 | tf_op jit(solution)/shard_map/ppermute | solution.py:281
  15.8 0.5 collective-permute-start.4
  16.3 0.8 collective-permute-done.14.refs_0_.refs_8_
  17.2 0.4 collective-permute-start.18
  17.7 1.4 %collective-permute-done.5.refs_6_.refs_14_ = bf16[32,2176]{1,0:T(8,128)(2,1)S(1)} collective-permute-done((bf16[32,2176]{1,0:T(8,128)(2,1)S(1)}, bf16[32,2176]{1,0:T(8,128)(2,1)S(1)}, u32[]{:S(2)}, u32[]{:S(2)}) %collective-permute-start.5) | collective-permute-done | bytes 139296 | tf_op jit(solution)/shard_map/ppermute | solution.py:281
  19.1 1.8 %collective-permute-start.16 = (bf16[32,2176]{1,0:T(8,128)(2,1)S(1)}, bf16[32,2176]{1,0:T(8,128)(2,1)S(1)}, u32[]{:S(2)}, u32[]{:S(2)}) collective-permute-start(bf16[32,2176]{1,0:T(8,128)(2,1)S(1)} %collective-permute-done.14.refs_0_.refs_8_), channel_id=1, source_target_pairs={{0,2},{1,3},{2,0},{3,1},{4,6},{5,7},{6,4},{7,5},{8,10},{9,11},{10,... | collective-permute-start | bytes 417800 | tf_op jit(solution)/shard_map/ppermute | solution.py:281
  20.9 1.4 %collective-permute-done.18.refs_4_.refs_12_ = bf16[32,2176]{1,0:T(8,128)(2,1)S(1)} collective-permute-done((bf16[32,2176]{1,0:T(8,128)(2,1)S(1)}, bf16[32,2176]{1,0:T(8,128)(2,1)S(1)}, u32[]{:S(2)}, u32[]{:S(2)}) %collective-permute-start.18) | collective-permute-done | bytes 139296 | tf_op jit(solution)/shard_map/ppermute | solution.py:281
  22.3 1.5 %collective-permute-start.20 = (bf16[32,2176]{1,0:T(8,128)(2,1)S(1)}, bf16[32,2176]{1,0:T(8,128)(2,1)S(1)}, u32[]{:S(2)}, u32[]{:S(2)}) collective-permute-start(bf16[32,2176]{1,0:T(8,128)(2,1)S(1)} %collective-permute-done.18.refs_4_.refs_12_), channel_id=1, source_target_pairs={{0,2},{1,3},{2,0},{3,1},{4,6},{5,7},{6,4},{7,5},{8,10},{9,11},{10,... | collective-permute-start | bytes 417800 | tf_op jit(solution)/shard_map/ppermute | solution.py:281
  23.8 1.9 %copy-done = bf16[1,2048,768]{2,1,0:T(8,128)(2,1)S(1)} copy-done((bf16[1,2048,768]{2,1,0:T(8,128)(2,1)S(1)}, bf16[1,2048,768]{2,1,0:T(8,128)(2,1)}, u32[]{:S(2)}) %copy-start) | copy-done | bytes 3145752
  25.7 1.9 %copy-done.2 = bf16[1,2048,768]{2,1,0:T(8,128)(2,1)S(1)} copy-done((bf16[1,2048,768]{2,1,0:T(8,128)(2,1)S(1)}, bf16[1,2048,768]{2,1,0:T(8,128)(2,1)}, u32[]{:S(2)}) %copy-start.2) | copy-done | bytes 3145752
  27.5 1.9 %copy-done.4 = bf16[1,768,2048]{2,1,0:T(8,128)(2,1)S(1)} copy-done((bf16[1,768,2048]{2,1,0:T(8,128)(2,1)S(1)}, bf16[1,768,2048]{2,1,0:T(8,128)(2,1)}, u32[]{:S(2)}) %copy-start.4) | copy-done | bytes 3145752
  29.4 2.7 %thinker.2 = (bf16[32,2048]{1,0:T(8,128)(2,1)S(1)}, bf16[32,2048]{1,0:T(8,128)(2,1)S(1)}, bf16[32,2048]{1,0:T(8,128)(2,1)S(1)}, bf16[32,2048]{1,0:T(8,128)(2,1)S...) custom-call(s32[1]{0:T(128)} %bitcast.expert_ref, ...), custom_call_target="tpu_custom_call" | custom-call | flops 2415919104 | bytes 9437184 | tf_op jit(solution)/shard_map/thinker/pallas_call | solution.py:222
  32.2 0.5 collective-permute-start.15
  34.4 0.5 collective-permute-start.9
  35.0 2.7 %thinker.3 = (bf16[32,2048]{1,0:T(8,128)(2,1)S(1)}, bf16[32,2048]{1,0:T(8,128)(2,1)S(1)}, bf16[32,2048]{1,0:T(8,128)(2,1)S(1)}, bf16[32,2048]{1,0:T(8,128)(2,1)S...) custom-call(s32[1]{0:T(128)} %bitcast.expert_ref, ...), custom_call_target="tpu_custom_call" | custom-call | flops 2415919104 | bytes 9437184 | tf_op jit(solution)/shard_map/thinker/pallas_call | solution.py:222
  38.4 0.7 collective-permute-done.26
  39.4 1.5 %collective-permute-start.27 = (bf16[32,2048]{1,0:T(8,128)(2,1)S(1)}, bf16[32,2048]{1,0:T(8,128)(2,1)S(1)}, u32[]{:S(2)}, u32[]{:S(2)}) collective-permute-start(bf16[32,2048]{1,0:T(8,128)(2,1)S(1)} %add_convert_fusion.2), channel_id=1, source_target_pairs={{0,2},{1,3},{2,0},{3,1},{4,6},{5,7},{6,4},{7,5},{8,10},{9,11},{10,... | collective-permute-start | bytes 393224 | tf_op jit(solution)/shard_map/ppermute | solution.py:281
  40.9 1.0 collective-permute-start.12
  42.0 3.8 %collective-permute-done.27 = bf16[32,2048]{1,0:T(8,128)(2,1)S(1)} collective-permute-done((bf16[32,2048]{1,0:T(8,128)(2,1)S(1)}, bf16[32,2048]{1,0:T(8,128)(2,1)S(1)}, u32[]{:S(2)}, u32[]{:S(2)}) %collective-permute-start.27) | collective-permute-done | bytes 131104 | tf_op jit(solution)/shard_map/ppermute | solution.py:281
  45.8 1.5 %collective-permute-start.24 = (bf16[32,2048]{1,0:T(8,128)(2,1)S(1)}, bf16[32,2048]{1,0:T(8,128)(2,1)S(1)}, u32[]{:S(2)}, u32[]{:S(2)}) collective-permute-start(bf16[32,2048]{1,0:T(8,128)(2,1)S(1)} %add_convert_fusion.3), channel_id=1, source_target_pairs={{0,2},{1,3},{2,0},{3,1},{4,6},{5,7},{6,4},{7,5},{8,10},{9,11},{10,... | collective-permute-start | bytes 393224 | tf_op jit(solution)/shard_map/ppermute | solution.py:281
  47.4 0.6 collective-permute-done.12
  48.0 0.4 collective-permute-start.28
  48.5 1.6 %collective-permute-start.13 = (bf16[32,2048]{1,0:T(8,128)(2,1)S(1)}, bf16[32,2048]{1,0:T(8,128)(2,1)S(1)}, u32[]{:S(2)}, u32[]{:S(2)}) collective-permute-start(bf16[32,2048]{1,0:T(8,128)(2,1)S(1)} %add_convert_fusion.4), channel_id=1, source_target_pairs={{0,4},{1,5},{2,6},{3,7},{4,0},{5,1},{6,2},{7,3},{8,12},{9,13},{10,... | collective-permute-start | bytes 393224 | tf_op jit(solution)/shard_map/ppermute | solution.py:281
  50.1 1.7 %collective-permute-done.24 = bf16[32,2048]{1,0:T(8,128)(2,1)S(1)} collective-permute-done((bf16[32,2048]{1,0:T(8,128)(2,1)S(1)}, bf16[32,2048]{1,0:T(8,128)(2,1)S(1)}, u32[]{:S(2)}, u32[]{:S(2)}) %collective-permute-start.24) | collective-permute-done | bytes 131104 | tf_op jit(solution)/shard_map/ppermute | solution.py:281
  51.8 2.5 %collective-permute-done.28 = bf16[32,2048]{1,0:T(8,128)(2,1)S(1)} collective-permute-done((bf16[32,2048]{1,0:T(8,128)(2,1)S(1)}, bf16[32,2048]{1,0:T(8,128)(2,1)S(1)}, u32[]{:S(2)}, u32[]{:S(2)}) %collective-permute-start.28) | collective-permute-done | bytes 131104 | tf_op jit(solution)/shard_map/ppermute | solution.py:281
  54.4 1.4 %collective-permute-start.29 = (bf16[32,2048]{1,0:T(8,128)(2,1)S(1)}, bf16[32,2048]{1,0:T(8,128)(2,1)S(1)}, u32[]{:S(2)}, u32[]{:S(2)}) collective-permute-start(bf16[32,2048]{1,0:T(8,128)(2,1)S(1)} %add_convert_fusion), channel_id=1, source_target_pairs={{0,8},{1,9},{2,10},{3,11},{4,12},{5,13},{6,14},{7,15},{8,0},{9,1},... | collective-permute-start | bytes 393224 | tf_op jit(solution)/shard_map/ppermute | solution.py:281
  56.2 5.4 %collective-permute-done.29.refs_4_ = bf16[32,2048]{1,0:T(8,128)(2,1)S(1)} collective-permute-done((bf16[32,2048]{1,0:T(8,128)(2,1)S(1)}, bf16[32,2048]{1,0:T(8,128)(2,1)S(1)}, u32[]{:S(2)}, u32[]{:S(2)}) %collective-permute-start.29) | collective-permute-done | bytes 131104 | tf_op jit(solution)/shard_map/ppermute | solution.py:281
  61.6 2.2 %copy-done.6 = bf16[2048,1024]{1,0:T(8,128)(2,1)S(1)} copy-done((bf16[2048,1024]{1,0:T(8,128)(2,1)S(1)}, bf16[2048,1024]{1,0:T(8,128)(2,1)}, u32[]{:S(2)}) %copy-start.6) | copy-done | bytes 4194328
  63.8 1.5 %relay.1 = (bf16[32,2048]{1,0:T(8,128)(2,1)}, bf16[32,1024]{1,0:T(8,128)(2,1)S(1)}) custom-call(bf16[32,2048]{1,0:T(8,128)(2,1)S(1)} %get-tuple-element.36.refs_0_, bf16[32,2048]{1,0:T(8,128)(2,1)S(1)} %collective-permute-done.7.refs_1_, bf16[32,2048]{1,0:T(8,128)(2,1)S(1)} %collective-permute-done.9.refs_2_, ...), custom_call_target="tpu_custom_call" | custom-call | flops 134217728 | bytes 4194304 | tf_op jit(solution)/shard_map/relay/pallas_call | solution.py:262
  65.5 2.8 %collective-permute-start.33 = (bf16[32,1024]{1,0:T(8,128)(2,1)S(1)}, bf16[32,1024]{1,0:T(8,128)(2,1)S(1)}, u32[]{:S(2)}, u32[]{:S(2)}) collective-permute-start(bf16[32,1024]{1,0:T(8,128)(2,1)S(1)} %get-tuple-element.53.refs_0_), channel_id=1, source_target_pairs={{0,4},{1,5},{2,6},{3,7},{4,0},{5,1},{6,2},{7,3},{8,12},{9,13},{10,... | collective-permute-start | bytes 196616 | tf_op jit(solution)/shard_map/ppermute | solution.py:281
  68.3 1.2 %collective-permute-start.31 = (bf16[32,1024]{1,0:T(8,128)(2,1)S(1)}, bf16[32,1024]{1,0:T(8,128)(2,1)S(1)}, u32[]{:S(2)}, u32[]{:S(2)}) collective-permute-start(bf16[32,1024]{1,0:T(8,128)(2,1)S(1)} %get-tuple-element.53.refs_0_), channel_id=1, source_target_pairs={{0,2},{1,3},{2,0},{3,1},{4,6},{5,7},{6,4},{7,5},{8,10},{9,11},{10,... | collective-permute-start | bytes 196616 | tf_op jit(solution)/shard_map/ppermute | solution.py:281
  69.4 1.3 %collective-permute-done.37.refs_8_ = bf16[32,1024]{1,0:T(8,128)(2,1)S(1)} collective-permute-done((bf16[32,1024]{1,0:T(8,128)(2,1)S(1)}, bf16[32,1024]{1,0:T(8,128)(2,1)S(1)}, u32[]{:S(2)}, u32[]{:S(2)}) %collective-permute-start.37) | collective-permute-done | bytes 65568 | tf_op jit(solution)/shard_map/ppermute | solution.py:281
  70.7 1.3 %collective-permute-start.39 = (bf16[32,1024]{1,0:T(8,128)(2,1)S(1)}, bf16[32,1024]{1,0:T(8,128)(2,1)S(1)}, u32[]{:S(2)}, u32[]{:S(2)}) collective-permute-start(bf16[32,1024]{1,0:T(8,128)(2,1)S(1)} %collective-permute-done.37.refs_8_), channel_id=1, source_target_pairs={{0,2},{1,3},{2,0},{3,1},{4,6},{5,7},{6,4},{7,5},{8,10},{9,11},{10,... | collective-permute-start | bytes 196616 | tf_op jit(solution)/shard_map/ppermute | solution.py:281
  72.1 0.5 collective-permute-done.31.refs_2_
  72.5 1.5 %collective-permute-start.35 = (bf16[32,1024]{1,0:T(8,128)(2,1)S(1)}, bf16[32,1024]{1,0:T(8,128)(2,1)S(1)}, u32[]{:S(2)}, u32[]{:S(2)}) collective-permute-start(bf16[32,1024]{1,0:T(8,128)(2,1)S(1)} %collective-permute-done.33.refs_4_), channel_id=1, source_target_pairs={{0,2},{1,3},{2,0},{3,1},{4,6},{5,7},{6,4},{7,5},{8,10},{9,11},{10,... | collective-permute-start | bytes 196616 | tf_op jit(solution)/shard_map/ppermute | solution.py:281
  74.0 1.0 collective-permute-done.41.refs_12_
  75.0 1.3 %collective-permute-start.43 = (bf16[32,1024]{1,0:T(8,128)(2,1)S(1)}, bf16[32,1024]{1,0:T(8,128)(2,1)S(1)}, u32[]{:S(2)}, u32[]{:S(2)}) collective-permute-start(bf16[32,1024]{1,0:T(8,128)(2,1)S(1)} %collective-permute-done.41.refs_12_), channel_id=1, source_target_pairs={{0,2},{1,3},{2,0},{3,1},{4,6},{5,7},{6,4},{7,5},{8,10},{9,11},{10,... | collective-permute-start | bytes 196616 | tf_op jit(solution)/shard_map/ppermute | solution.py:281
  76.3 0.5 collective-permute-start.42
  76.9 0.4 collective-permute-start.36
  77.4 1.9 %collective-permute-done.43.refs_14_ = bf16[32,1024]{1,0:T(8,128)(2,1)S(1)} collective-permute-done((bf16[32,1024]{1,0:T(8,128)(2,1)S(1)}, bf16[32,1024]{1,0:T(8,128)(2,1)S(1)}, u32[]{:S(2)}, u32[]{:S(2)}) %collective-permute-start.43) | collective-permute-done | bytes 65568 | tf_op jit(solution)/shard_map/ppermute | solution.py:281
  79.5 1.1 collective-permute-done.44.refs_15_
  80.5 2.4 %talker.1 = (bf16[32,1024]{1,0:T(8,128)(2,1)S(1)}, bf16[32,1024]{1,0:T(8,128)(2,1)S(1)}, bf16[32,1024]{1,0:T(8,128)(2,1)S(1)}, bf16[32,1024]{1,0:T(8,128)(2,1)S(...) custom-call(s32[1]{0:T(128)} %bitcast.expert_ref, ...), custom_call_target="tpu_custom_call" | custom-call | flops 1207959552 | bytes 2359296 | tf_op jit(solution)/shard_map/talker/pallas_call | solution.py:222
  85.3 0.9 collective-permute-done.56
  86.6 1.4 %collective-permute-start.57 = (bf16[32,1024]{1,0:T(8,128)(2,1)S(1)}, bf16[32,1024]{1,0:T(8,128)(2,1)S(1)}, u32[]{:S(2)}, u32[]{:S(2)}) collective-permute-start(bf16[32,1024]{1,0:T(8,128)(2,1)S(1)} %add_convert_fusion.10), channel_id=1, source_target_pairs={{0,2},{1,3},{2,0},{3,1},{4,6},{5,7},{6,4},{7,5},{8,10},{9,11},{10,... | collective-permute-start | bytes 196616 | tf_op jit(solution)/shard_map/ppermute | solution.py:281
  88.0 0.8 collective-permute-start.47
  88.8 2.5 %collective-permute-done.57 = bf16[32,1024]{1,0:T(8,128)(2,1)S(1)} collective-permute-done((bf16[32,1024]{1,0:T(8,128)(2,1)S(1)}, bf16[32,1024]{1,0:T(8,128)(2,1)S(1)}, u32[]{:S(2)}, u32[]{:S(2)}) %collective-permute-start.57) | collective-permute-done | bytes 65568 | tf_op jit(solution)/shard_map/ppermute | solution.py:281
  91.3 1.5 %collective-permute-start.50 = (bf16[32,1024]{1,0:T(8,128)(2,1)S(1)}, bf16[32,1024]{1,0:T(8,128)(2,1)S(1)}, u32[]{:S(2)}, u32[]{:S(2)}) collective-permute-start(bf16[32,1024]{1,0:T(8,128)(2,1)S(1)} %add_convert_fusion.13), channel_id=1, source_target_pairs={{0,2},{1,3},{2,0},{3,1},{4,6},{5,7},{6,4},{7,5},{8,10},{9,11},{10,... | collective-permute-start | bytes 196616 | tf_op jit(solution)/shard_map/ppermute | solution.py:281
  92.8 0.6 collective-permute-start.54
  93.4 2.1 %collective-permute-done.50 = bf16[32,1024]{1,0:T(8,128)(2,1)S(1)} collective-permute-done((bf16[32,1024]{1,0:T(8,128)(2,1)S(1)}, bf16[32,1024]{1,0:T(8,128)(2,1)S(1)}, u32[]{:S(2)}, u32[]{:S(2)}) %collective-permute-start.50) | collective-permute-done | bytes 65568 | tf_op jit(solution)/shard_map/ppermute | solution.py:281
  95.5 0.9 collective-permute-start.58
  96.4 1.2 %collective-permute-start.51 = (bf16[32,1024]{1,0:T(8,128)(2,1)S(1)}, bf16[32,1024]{1,0:T(8,128)(2,1)S(1)}, u32[]{:S(2)}, u32[]{:S(2)}) collective-permute-start(bf16[32,1024]{1,0:T(8,128)(2,1)S(1)} %add_convert_fusion.12), channel_id=1, source_target_pairs={{0,4},{1,5},{2,6},{3,7},{4,0},{5,1},{6,2},{7,3},{8,12},{9,13},{10,... | collective-permute-start | bytes 196616 | tf_op jit(solution)/shard_map/ppermute | solution.py:281
  97.7 2.1 %collective-permute-done.58 = bf16[32,1024]{1,0:T(8,128)(2,1)S(1)} collective-permute-done((bf16[32,1024]{1,0:T(8,128)(2,1)S(1)}, bf16[32,1024]{1,0:T(8,128)(2,1)S(1)}, u32[]{:S(2)}, u32[]{:S(2)}) %collective-permute-start.58) | collective-permute-done | bytes 65568 | tf_op jit(solution)/shard_map/ppermute | solution.py:281
  99.8 2.0 %collective-permute-start.59 = (bf16[32,1024]{1,0:T(8,128)(2,1)S(1)}, bf16[32,1024]{1,0:T(8,128)(2,1)S(1)}, u32[]{:S(2)}, u32[]{:S(2)}) collective-permute-start(bf16[32,1024]{1,0:T(8,128)(2,1)S(1)} %add_convert_fusion.8), channel_id=1, source_target_pairs={{0,8},{1,9},{2,10},{3,11},{4,12},{5,13},{6,14},{7,15},{8,0},{9,1},... | collective-permute-start | bytes 196616 | tf_op jit(solution)/shard_map/ppermute | solution.py:281
  101.9 3.9 %collective-permute-done.59 = bf16[32,1024]{1,0:T(8,128)(2,1)S(1)} collective-permute-done((bf16[32,1024]{1,0:T(8,128)(2,1)S(1)}, bf16[32,1024]{1,0:T(8,128)(2,1)S(1)}, u32[]{:S(2)}, u32[]{:S(2)}) %collective-permute-start.59) | collective-permute-done | bytes 65568 | tf_op jit(solution)/shard_map/ppermute | solution.py:281
  105.8 0.7 add_convert_fusion.7
  (123 shorter events, 6.9 us)
Async XLA Ops:
  5.0 9.0 %collective-permute-start.3 = (bf16[32,2176]{1,0:T(8,128)(2,1)S(1)}, bf16[32,2176]{1,0:T(8,128)(2,1)S(1)}, u32[]{:S(2)}, u32[]{:S(2)}) collective-permute-start(bf16[32,2176]{1,0:T(8,128)(2,1)S(1)} %pack.1.refs_0_.refs_8_), channel_id=1, source_target_pairs={{0,4},{1,5},{2,6},{3,7},{4,0},{5,1},{6,2},{7,3},{8,12},{9,13},{10,... | collective-permute-start | bytes 417800 | tf_op jit(solution)/shard_map/ppermute | solution.py:281
  8.1 9.1 %collective-permute-start.14 = (bf16[32,2176]{1,0:T(8,128)(2,1)S(1)}, bf16[32,2176]{1,0:T(8,128)(2,1)S(1)}, u32[]{:S(2)}, u32[]{:S(2)}) collective-permute-start(bf16[32,2176]{1,0:T(8,128)(2,1)S(1)} %pack.1.refs_0_.refs_8_), channel_id=1, source_target_pairs={{0,8},{1,9},{2,10},{3,11},{4,12},{5,13},{6,14},{7,15},{8,0},{9,1},... | collective-permute-start | bytes 417800 | tf_op jit(solution)/shard_map/ppermute | solution.py:281
  10.7 6.9 %collective-permute-start.1 = (bf16[32,2176]{1,0:T(8,128)(2,1)S(1)}, bf16[32,2176]{1,0:T(8,128)(2,1)S(1)}, u32[]{:S(2)}, u32[]{:S(2)}) collective-permute-start(bf16[32,2176]{1,0:T(8,128)(2,1)S(1)} %pack.1.refs_0_.refs_8_), channel_id=1, source_target_pairs={{0,2},{1,3},{2,0},{3,1},{4,6},{5,7},{6,4},{7,5},{8,10},{9,11},{10,... | collective-permute-start | bytes 417800 | tf_op jit(solution)/shard_map/ppermute | solution.py:281
  14.0 5.1 %collective-permute-start.5 = (bf16[32,2176]{1,0:T(8,128)(2,1)S(1)}, bf16[32,2176]{1,0:T(8,128)(2,1)S(1)}, u32[]{:S(2)}, u32[]{:S(2)}) collective-permute-start(bf16[32,2176]{1,0:T(8,128)(2,1)S(1)} %collective-permute-done.3.refs_4_.refs_12_), channel_id=1, source_target_pairs={{0,2},{1,3},{2,0},{3,1},{4,6},{5,7},{6,4},{7,5},{8,10},{9,11},{10,... | collective-permute-start | bytes 417800 | tf_op jit(solution)/shard_map/ppermute | solution.py:281
  15.8 3.2 %collective-permute-start = (bf16[32,2176]{1,0:T(8,128)(2,1)S(1)}, bf16[32,2176]{1,0:T(8,128)(2,1)S(1)}, u32[]{:S(2)}, u32[]{:S(2)}) collective-permute-start(bf16[32,2176]{1,0:T(8,128)(2,1)S(1)} %pack.1.refs_0_.refs_8_), channel_id=1, source_target_pairs={{0,1},{1,0},{2,3},{3,2},{4,5},{5,4},{6,7},{7,6},{8,9},{9,8},{10,11... | collective-permute-start | bytes 417800 | tf_op jit(solution)/shard_map/ppermute | solution.py:281
  15.8 7.9 %collective-permute-start.4 = (bf16[32,2176]{1,0:T(8,128)(2,1)S(1)}, bf16[32,2176]{1,0:T(8,128)(2,1)S(1)}, u32[]{:S(2)}, u32[]{:S(2)}) collective-permute-start(bf16[32,2176]{1,0:T(8,128)(2,1)S(1)} %collective-permute-done.3.refs_4_.refs_12_), channel_id=1, source_target_pairs={{0,1},{1,0},{2,3},{3,2},{4,5},{5,4},{6,7},{7,6},{8,9},{9,8},{10,11... | collective-permute-start | bytes 417800 | tf_op jit(solution)/shard_map/ppermute | solution.py:281
  17.2 5.1 %collective-permute-start.18 = (bf16[32,2176]{1,0:T(8,128)(2,1)S(1)}, bf16[32,2176]{1,0:T(8,128)(2,1)S(1)}, u32[]{:S(2)}, u32[]{:S(2)}) collective-permute-start(bf16[32,2176]{1,0:T(8,128)(2,1)S(1)} %collective-permute-done.14.refs_0_.refs_8_), channel_id=1, source_target_pairs={{0,4},{1,5},{2,6},{3,7},{4,0},{5,1},{6,2},{7,3},{8,12},{9,13},{10,... | collective-permute-start | bytes 417800 | tf_op jit(solution)/shard_map/ppermute | solution.py:281
  17.6 6.1 %collective-permute-start.2 = (bf16[32,2176]{1,0:T(8,128)(2,1)S(1)}, bf16[32,2176]{1,0:T(8,128)(2,1)S(1)}, u32[]{:S(2)}, u32[]{:S(2)}) collective-permute-start(bf16[32,2176]{1,0:T(8,128)(2,1)S(1)} %collective-permute-done.1.refs_2_.refs_10_), channel_id=1, source_target_pairs={{0,1},{1,0},{2,3},{3,2},{4,5},{5,4},{6,7},{7,6},{8,9},{9,8},{10,11... | collective-permute-start | bytes 417800 | tf_op jit(solution)/shard_map/ppermute | solution.py:281
  19.1 4.7 %collective-permute-start.6 = (bf16[32,2176]{1,0:T(8,128)(2,1)S(1)}, bf16[32,2176]{1,0:T(8,128)(2,1)S(1)}, u32[]{:S(2)}, u32[]{:S(2)}) collective-permute-start(bf16[32,2176]{1,0:T(8,128)(2,1)S(1)} %collective-permute-done.5.refs_6_.refs_14_), channel_id=1, source_target_pairs={{0,1},{1,0},{2,3},{3,2},{4,5},{5,4},{6,7},{7,6},{8,9},{9,8},{10,11... | collective-permute-start | bytes 417800 | tf_op jit(solution)/shard_map/ppermute | solution.py:281
  19.1 13.7 %collective-permute-start.16 = (bf16[32,2176]{1,0:T(8,128)(2,1)S(1)}, bf16[32,2176]{1,0:T(8,128)(2,1)S(1)}, u32[]{:S(2)}, u32[]{:S(2)}) collective-permute-start(bf16[32,2176]{1,0:T(8,128)(2,1)S(1)} %collective-permute-done.14.refs_0_.refs_8_), channel_id=1, source_target_pairs={{0,2},{1,3},{2,0},{3,1},{4,6},{5,7},{6,4},{7,5},{8,10},{9,11},{10,... | collective-permute-start | bytes 417800 | tf_op jit(solution)/shard_map/ppermute | solution.py:281
  22.3 11.0 %collective-permute-start.20 = (bf16[32,2176]{1,0:T(8,128)(2,1)S(1)}, bf16[32,2176]{1,0:T(8,128)(2,1)S(1)}, u32[]{:S(2)}, u32[]{:S(2)}) collective-permute-start(bf16[32,2176]{1,0:T(8,128)(2,1)S(1)} %collective-permute-done.18.refs_4_.refs_12_), channel_id=1, source_target_pairs={{0,2},{1,3},{2,0},{3,1},{4,6},{5,7},{6,4},{7,5},{8,10},{9,11},{10,... | collective-permute-start | bytes 417800 | tf_op jit(solution)/shard_map/ppermute | solution.py:281
  32.2 1.4 %collective-permute-start.8 = (bf16[32,2048]{1,0:T(8,128)(2,1)S(1)}, bf16[32,2048]{1,0:T(8,128)(2,1)S(1)}, u32[]{:S(2)}, u32[]{:S(2)}) collective-permute-start(bf16[32,2048]{1,0:T(8,128)(2,1)S(1)} %get-tuple-element.39), channel_id=1, source_target_pairs={{0,1},{1,0},{2,3},{3,2},{4,5},{5,4},{6,7},{7,6},{8,9},{9,8},{10,11... | collective-permute-start | bytes 393224 | tf_op jit(solution)/shard_map/ppermute | solution.py:281
  32.2 1.6 %collective-permute-start.15 = (bf16[32,2176]{1,0:T(8,128)(2,1)S(1)}, bf16[32,2176]{1,0:T(8,128)(2,1)S(1)}, u32[]{:S(2)}, u32[]{:S(2)}) collective-permute-start(bf16[32,2176]{1,0:T(8,128)(2,1)S(1)} %collective-permute-done.14.refs_0_.refs_8_), channel_id=1, source_target_pairs={{0,1},{1,0},{2,3},{3,2},{4,5},{5,4},{6,7},{7,6},{8,9},{9,8},{10,11... | collective-permute-start | bytes 417800 | tf_op jit(solution)/shard_map/ppermute | solution.py:281
  32.7 1.5 %collective-permute-start.19 = (bf16[32,2176]{1,0:T(8,128)(2,1)S(1)}, bf16[32,2176]{1,0:T(8,128)(2,1)S(1)}, u32[]{:S(2)}, u32[]{:S(2)}) collective-permute-start(bf16[32,2176]{1,0:T(8,128)(2,1)S(1)} %collective-permute-done.18.refs_4_.refs_12_), channel_id=1, source_target_pairs={{0,1},{1,0},{2,3},{3,2},{4,5},{5,4},{6,7},{7,6},{8,9},{9,8},{10,11... | collective-permute-start | bytes 417800 | tf_op jit(solution)/shard_map/ppermute | solution.py:281
  32.8 1.6 %collective-permute-start.17 = (bf16[32,2176]{1,0:T(8,128)(2,1)S(1)}, bf16[32,2176]{1,0:T(8,128)(2,1)S(1)}, u32[]{:S(2)}, u32[]{:S(2)}) collective-permute-start(bf16[32,2176]{1,0:T(8,128)(2,1)S(1)} %collective-permute-done.16.refs_2_.refs_10_), channel_id=1, source_target_pairs={{0,1},{1,0},{2,3},{3,2},{4,5},{5,4},{6,7},{7,6},{8,9},{9,8},{10,11... | collective-permute-start | bytes 417800 | tf_op jit(solution)/shard_map/ppermute | solution.py:281
  33.3 22.6 %collective-permute-start.7 = (bf16[32,2048]{1,0:T(8,128)(2,1)S(1)}, bf16[32,2048]{1,0:T(8,128)(2,1)S(1)}, u32[]{:S(2)}, u32[]{:S(2)}) collective-permute-start(bf16[32,2048]{1,0:T(8,128)(2,1)S(1)} %get-tuple-element.37), channel_id=1, source_target_pairs={{0,1},{1,0},{2,3},{3,2},{4,5},{5,4},{6,7},{7,6},{8,9},{9,8},{10,11... | collective-permute-start | bytes 393224 | tf_op jit(solution)/shard_map/ppermute | solution.py:281
  33.6 1.4 %collective-permute-start.21 = (bf16[32,2176]{1,0:T(8,128)(2,1)S(1)}, bf16[32,2176]{1,0:T(8,128)(2,1)S(1)}, u32[]{:S(2)}, u32[]{:S(2)}) collective-permute-start(bf16[32,2176]{1,0:T(8,128)(2,1)S(1)} %collective-permute-done.20.refs_6_.refs_14_), channel_id=1, source_target_pairs={{0,1},{1,0},{2,3},{3,2},{4,5},{5,4},{6,7},{7,6},{8,9},{9,8},{10,11... | collective-permute-start | bytes 417800 | tf_op jit(solution)/shard_map/ppermute | solution.py:281
  33.8 12.0 %collective-permute-start.10 = (bf16[32,2048]{1,0:T(8,128)(2,1)S(1)}, bf16[32,2048]{1,0:T(8,128)(2,1)S(1)}, u32[]{:S(2)}, u32[]{:S(2)}) collective-permute-start(bf16[32,2048]{1,0:T(8,128)(2,1)S(1)} %get-tuple-element.41), channel_id=1, source_target_pairs={{0,1},{1,0},{2,3},{3,2},{4,5},{5,4},{6,7},{7,6},{8,9},{9,8},{10,11... | collective-permute-start | bytes 393224 | tf_op jit(solution)/shard_map/ppermute | solution.py:281
  34.2 21.6 %copy-start.12 = (s32[32]{0:T(128)S(1)}, s32[32]{0:T(128)}, u32[]{:S(2)}) copy-start(s32[32]{0:T(128)} %param.21) | copy-start | bytes 388
  34.2 27.4 %copy-start.8 = (f32[1024]{0:T(1024)S(1)}, f32[1024]{0:T(1024)}, u32[]{:S(2)}) copy-start(f32[1024]{0:T(1024)} %param.22) | copy-start | bytes 12292
  34.2 3.7 %collective-permute-start.11 = (bf16[32,2048]{1,0:T(8,128)(2,1)S(1)}, bf16[32,2048]{1,0:T(8,128)(2,1)S(1)}, u32[]{:S(2)}, u32[]{:S(2)}) collective-permute-start(bf16[32,2048]{1,0:T(8,128)(2,1)S(1)} %get-tuple-element.43), channel_id=1, source_target_pairs={{0,1},{1,0},{2,3},{3,2},{4,5},{5,4},{6,7},{7,6},{8,9},{9,8},{10,11... | collective-permute-start | bytes 393224 | tf_op jit(solution)/shard_map/ppermute | solution.py:281
  34.4 21.5 %collective-permute-start.9 = (bf16[32,2048]{1,0:T(8,128)(2,1)S(1)}, bf16[32,2048]{1,0:T(8,128)(2,1)S(1)}, u32[]{:S(2)}, u32[]{:S(2)}) collective-permute-start(bf16[32,2048]{1,0:T(8,128)(2,1)S(1)} %add_convert_fusion.6), channel_id=1, source_target_pairs={{0,2},{1,3},{2,0},{3,1},{4,6},{5,7},{6,4},{7,5},{8,10},{9,11},{10,... | collective-permute-start | bytes 393224 | tf_op jit(solution)/shard_map/ppermute | solution.py:281
  37.7 1.4 %collective-permute-start.26 = (bf16[32,2048]{1,0:T(8,128)(2,1)S(1)}, bf16[32,2048]{1,0:T(8,128)(2,1)S(1)}, u32[]{:S(2)}, u32[]{:S(2)}) collective-permute-start(bf16[32,2048]{1,0:T(8,128)(2,1)S(1)} %get-tuple-element.51), channel_id=1, source_target_pairs={{0,1},{1,0},{2,3},{3,2},{4,5},{5,4},{6,7},{7,6},{8,9},{9,8},{10,11... | collective-permute-start | bytes 393224 | tf_op jit(solution)/shard_map/ppermute | solution.py:281
  38.0 1.4 %collective-permute-start.23 = (bf16[32,2048]{1,0:T(8,128)(2,1)S(1)}, bf16[32,2048]{1,0:T(8,128)(2,1)S(1)}, u32[]{:S(2)}, u32[]{:S(2)}) collective-permute-start(bf16[32,2048]{1,0:T(8,128)(2,1)S(1)} %get-tuple-element.47), channel_id=1, source_target_pairs={{0,1},{1,0},{2,3},{3,2},{4,5},{5,4},{6,7},{7,6},{8,9},{9,8},{10,11... | collective-permute-start | bytes 393224 | tf_op jit(solution)/shard_map/ppermute | solution.py:281
  39.1 1.8 %collective-permute-start.25 = (bf16[32,2048]{1,0:T(8,128)(2,1)S(1)}, bf16[32,2048]{1,0:T(8,128)(2,1)S(1)}, u32[]{:S(2)}, u32[]{:S(2)}) collective-permute-start(bf16[32,2048]{1,0:T(8,128)(2,1)S(1)} %get-tuple-element.49), channel_id=1, source_target_pairs={{0,1},{1,0},{2,3},{3,2},{4,5},{5,4},{6,7},{7,6},{8,9},{9,8},{10,11... | collective-permute-start | bytes 393224 | tf_op jit(solution)/shard_map/ppermute | solution.py:281
  39.4 6.4 %collective-permute-start.27 = (bf16[32,2048]{1,0:T(8,128)(2,1)S(1)}, bf16[32,2048]{1,0:T(8,128)(2,1)S(1)}, u32[]{:S(2)}, u32[]{:S(2)}) collective-permute-start(bf16[32,2048]{1,0:T(8,128)(2,1)S(1)} %add_convert_fusion.2), channel_id=1, source_target_pairs={{0,2},{1,3},{2,0},{3,1},{4,6},{5,7},{6,4},{7,5},{8,10},{9,11},{10,... | collective-permute-start | bytes 393224 | tf_op jit(solution)/shard_map/ppermute | solution.py:281
  40.9 7.0 %collective-permute-start.12 = (bf16[32,2048]{1,0:T(8,128)(2,1)S(1)}, bf16[32,2048]{1,0:T(8,128)(2,1)S(1)}, u32[]{:S(2)}, u32[]{:S(2)}) collective-permute-start(bf16[32,2048]{1,0:T(8,128)(2,1)S(1)} %add_convert_fusion.5), channel_id=1, source_target_pairs={{0,2},{1,3},{2,0},{3,1},{4,6},{5,7},{6,4},{7,5},{8,10},{9,11},{10,... | collective-permute-start | bytes 393224 | tf_op jit(solution)/shard_map/ppermute | solution.py:281
  45.8 2.7 %collective-permute-start.22 = (bf16[32,2048]{1,0:T(8,128)(2,1)S(1)}, bf16[32,2048]{1,0:T(8,128)(2,1)S(1)}, u32[]{:S(2)}, u32[]{:S(2)}) collective-permute-start(bf16[32,2048]{1,0:T(8,128)(2,1)S(1)} %get-tuple-element.45), channel_id=1, source_target_pairs={{0,1},{1,0},{2,3},{3,2},{4,5},{5,4},{6,7},{7,6},{8,9},{9,8},{10,11... | collective-permute-start | bytes 393224 | tf_op jit(solution)/shard_map/ppermute | solution.py:281
  45.8 6.0 %collective-permute-start.24 = (bf16[32,2048]{1,0:T(8,128)(2,1)S(1)}, bf16[32,2048]{1,0:T(8,128)(2,1)S(1)}, u32[]{:S(2)}, u32[]{:S(2)}) collective-permute-start(bf16[32,2048]{1,0:T(8,128)(2,1)S(1)} %add_convert_fusion.3), channel_id=1, source_target_pairs={{0,2},{1,3},{2,0},{3,1},{4,6},{5,7},{6,4},{7,5},{8,10},{9,11},{10,... | collective-permute-start | bytes 393224 | tf_op jit(solution)/shard_map/ppermute | solution.py:281
  48.0 6.4 %collective-permute-start.28 = (bf16[32,2048]{1,0:T(8,128)(2,1)S(1)}, bf16[32,2048]{1,0:T(8,128)(2,1)S(1)}, u32[]{:S(2)}, u32[]{:S(2)}) collective-permute-start(bf16[32,2048]{1,0:T(8,128)(2,1)S(1)} %add_convert_fusion.1), channel_id=1, source_target_pairs={{0,4},{1,5},{2,6},{3,7},{4,0},{5,1},{6,2},{7,3},{8,12},{9,13},{10,... | collective-permute-start | bytes 393224 | tf_op jit(solution)/shard_map/ppermute | solution.py:281
  48.5 7.7 %collective-permute-start.13 = (bf16[32,2048]{1,0:T(8,128)(2,1)S(1)}, bf16[32,2048]{1,0:T(8,128)(2,1)S(1)}, u32[]{:S(2)}, u32[]{:S(2)}) collective-permute-start(bf16[32,2048]{1,0:T(8,128)(2,1)S(1)} %add_convert_fusion.4), channel_id=1, source_target_pairs={{0,4},{1,5},{2,6},{3,7},{4,0},{5,1},{6,2},{7,3},{8,12},{9,13},{10,... | collective-permute-start | bytes 393224 | tf_op jit(solution)/shard_map/ppermute | solution.py:281
  54.4 7.2 %collective-permute-start.29 = (bf16[32,2048]{1,0:T(8,128)(2,1)S(1)}, bf16[32,2048]{1,0:T(8,128)(2,1)S(1)}, u32[]{:S(2)}, u32[]{:S(2)}) collective-permute-start(bf16[32,2048]{1,0:T(8,128)(2,1)S(1)} %add_convert_fusion), channel_id=1, source_target_pairs={{0,8},{1,9},{2,10},{3,11},{4,12},{5,13},{6,14},{7,15},{8,0},{9,1},... | collective-permute-start | bytes 393224 | tf_op jit(solution)/shard_map/ppermute | solution.py:281
  63.8 16.7 %copy-start.10 = (bf16[1,1024,384]{2,1,0:T(8,128)(2,1)S(1)}, bf16[1,1024,384]{2,1,0:T(8,128)(2,1)}, u32[]{:S(2)}) copy-start(bf16[1,1024,384]{2,1,0:T(8,128)(2,1)} %refs_33_.1) | copy-start | bytes 2359300
  63.8 16.7 %copy-start.11 = (bf16[1,384,1024]{2,1,0:T(8,128)(2,1)S(1)}, bf16[1,384,1024]{2,1,0:T(8,128)(2,1)}, u32[]{:S(2)}) copy-start(bf16[1,384,1024]{2,1,0:T(8,128)(2,1)} %refs_34_.1) | copy-start | bytes 2359300
  65.3 5.4 %collective-permute-start.37 = (bf16[32,1024]{1,0:T(8,128)(2,1)S(1)}, bf16[32,1024]{1,0:T(8,128)(2,1)S(1)}, u32[]{:S(2)}, u32[]{:S(2)}) collective-permute-start(bf16[32,1024]{1,0:T(8,128)(2,1)S(1)} %get-tuple-element.53.refs_0_), channel_id=1, source_target_pairs={{0,8},{1,9},{2,10},{3,11},{4,12},{5,13},{6,14},{7,15},{8,0},{9,1},... | collective-permute-start | bytes 196616 | tf_op jit(solution)/shard_map/ppermute | solution.py:281
  65.5 6.6 %collective-permute-start.33 = (bf16[32,1024]{1,0:T(8,128)(2,1)S(1)}, bf16[32,1024]{1,0:T(8,128)(2,1)S(1)}, u32[]{:S(2)}, u32[]{:S(2)}) collective-permute-start(bf16[32,1024]{1,0:T(8,128)(2,1)S(1)} %get-tuple-element.53.refs_0_), channel_id=1, source_target_pairs={{0,4},{1,5},{2,6},{3,7},{4,0},{5,1},{6,2},{7,3},{8,12},{9,13},{10,... | collective-permute-start | bytes 196616 | tf_op jit(solution)/shard_map/ppermute | solution.py:281
  68.3 4.3 %collective-permute-start.31 = (bf16[32,1024]{1,0:T(8,128)(2,1)S(1)}, bf16[32,1024]{1,0:T(8,128)(2,1)S(1)}, u32[]{:S(2)}, u32[]{:S(2)}) collective-permute-start(bf16[32,1024]{1,0:T(8,128)(2,1)S(1)} %get-tuple-element.53.refs_0_), channel_id=1, source_target_pairs={{0,2},{1,3},{2,0},{3,1},{4,6},{5,7},{6,4},{7,5},{8,10},{9,11},{10,... | collective-permute-start | bytes 196616 | tf_op jit(solution)/shard_map/ppermute | solution.py:281
  69.4 4.6 %collective-permute-start.30 = (bf16[32,1024]{1,0:T(8,128)(2,1)S(1)}, bf16[32,1024]{1,0:T(8,128)(2,1)S(1)}, u32[]{:S(2)}, u32[]{:S(2)}) collective-permute-start(bf16[32,1024]{1,0:T(8,128)(2,1)S(1)} %get-tuple-element.53.refs_0_), channel_id=1, source_target_pairs={{0,1},{1,0},{2,3},{3,2},{4,5},{5,4},{6,7},{7,6},{8,9},{9,8},{10,11... | collective-permute-start | bytes 196616 | tf_op jit(solution)/shard_map/ppermute | solution.py:281
  70.7 4.3 %collective-permute-start.41 = (bf16[32,1024]{1,0:T(8,128)(2,1)S(1)}, bf16[32,1024]{1,0:T(8,128)(2,1)S(1)}, u32[]{:S(2)}, u32[]{:S(2)}) collective-permute-start(bf16[32,1024]{1,0:T(8,128)(2,1)S(1)} %collective-permute-done.37.refs_8_), channel_id=1, source_target_pairs={{0,4},{1,5},{2,6},{3,7},{4,0},{5,1},{6,2},{7,3},{8,12},{9,13},{10,... | collective-permute-start | bytes 196616 | tf_op jit(solution)/shard_map/ppermute | solution.py:281
  70.7 5.6 %collective-permute-start.39 = (bf16[32,1024]{1,0:T(8,128)(2,1)S(1)}, bf16[32,1024]{1,0:T(8,128)(2,1)S(1)}, u32[]{:S(2)}, u32[]{:S(2)}) collective-permute-start(bf16[32,1024]{1,0:T(8,128)(2,1)S(1)} %collective-permute-done.37.refs_8_), channel_id=1, source_target_pairs={{0,2},{1,3},{2,0},{3,1},{4,6},{5,7},{6,4},{7,5},{8,10},{9,11},{10,... | collective-permute-start | bytes 196616 | tf_op jit(solution)/shard_map/ppermute | solution.py:281
  72.1 4.3 %collective-permute-start.38 = (bf16[32,1024]{1,0:T(8,128)(2,1)S(1)}, bf16[32,1024]{1,0:T(8,128)(2,1)S(1)}, u32[]{:S(2)}, u32[]{:S(2)}) collective-permute-start(bf16[32,1024]{1,0:T(8,128)(2,1)S(1)} %collective-permute-done.37.refs_8_), channel_id=1, source_target_pairs={{0,1},{1,0},{2,3},{3,2},{4,5},{5,4},{6,7},{7,6},{8,9},{9,8},{10,11... | collective-permute-start | bytes 196616 | tf_op jit(solution)/shard_map/ppermute | solution.py:281
  72.5 4.3 %collective-permute-start.35 = (bf16[32,1024]{1,0:T(8,128)(2,1)S(1)}, bf16[32,1024]{1,0:T(8,128)(2,1)S(1)}, u32[]{:S(2)}, u32[]{:S(2)}) collective-permute-start(bf16[32,1024]{1,0:T(8,128)(2,1)S(1)} %collective-permute-done.33.refs_4_), channel_id=1, source_target_pairs={{0,2},{1,3},{2,0},{3,1},{4,6},{5,7},{6,4},{7,5},{8,10},{9,11},{10,... | collective-permute-start | bytes 196616 | tf_op jit(solution)/shard_map/ppermute | solution.py:281
  74.0 2.9 %collective-permute-start.34 = (bf16[32,1024]{1,0:T(8,128)(2,1)S(1)}, bf16[32,1024]{1,0:T(8,128)(2,1)S(1)}, u32[]{:S(2)}, u32[]{:S(2)}) collective-permute-start(bf16[32,1024]{1,0:T(8,128)(2,1)S(1)} %collective-permute-done.33.refs_4_), channel_id=1, source_target_pairs={{0,1},{1,0},{2,3},{3,2},{4,5},{5,4},{6,7},{7,6},{8,9},{9,8},{10,11... | collective-permute-start | bytes 196616 | tf_op jit(solution)/shard_map/ppermute | solution.py:281
  75.0 4.3 %collective-permute-start.43 = (bf16[32,1024]{1,0:T(8,128)(2,1)S(1)}, bf16[32,1024]{1,0:T(8,128)(2,1)S(1)}, u32[]{:S(2)}, u32[]{:S(2)}) collective-permute-start(bf16[32,1024]{1,0:T(8,128)(2,1)S(1)} %collective-permute-done.41.refs_12_), channel_id=1, source_target_pairs={{0,2},{1,3},{2,0},{3,1},{4,6},{5,7},{6,4},{7,5},{8,10},{9,11},{10,... | collective-permute-start | bytes 196616 | tf_op jit(solution)/shard_map/ppermute | solution.py:281
  76.3 3.1 %collective-permute-start.32 = (bf16[32,1024]{1,0:T(8,128)(2,1)S(1)}, bf16[32,1024]{1,0:T(8,128)(2,1)S(1)}, u32[]{:S(2)}, u32[]{:S(2)}) collective-permute-start(bf16[32,1024]{1,0:T(8,128)(2,1)S(1)} %collective-permute-done.31.refs_2_), channel_id=1, source_target_pairs={{0,1},{1,0},{2,3},{3,2},{4,5},{5,4},{6,7},{7,6},{8,9},{9,8},{10,11... | collective-permute-start | bytes 196616 | tf_op jit(solution)/shard_map/ppermute | solution.py:281
  76.3 3.1 %collective-permute-start.42 = (bf16[32,1024]{1,0:T(8,128)(2,1)S(1)}, bf16[32,1024]{1,0:T(8,128)(2,1)S(1)}, u32[]{:S(2)}, u32[]{:S(2)}) collective-permute-start(bf16[32,1024]{1,0:T(8,128)(2,1)S(1)} %collective-permute-done.41.refs_12_), channel_id=1, source_target_pairs={{0,1},{1,0},{2,3},{3,2},{4,5},{5,4},{6,7},{7,6},{8,9},{9,8},{10,11... | collective-permute-start | bytes 196616 | tf_op jit(solution)/shard_map/ppermute | solution.py:281
  76.8 2.6 %collective-permute-start.40 = (bf16[32,1024]{1,0:T(8,128)(2,1)S(1)}, bf16[32,1024]{1,0:T(8,128)(2,1)S(1)}, u32[]{:S(2)}, u32[]{:S(2)}) collective-permute-start(bf16[32,1024]{1,0:T(8,128)(2,1)S(1)} %collective-permute-done.39.refs_10_), channel_id=1, source_target_pairs={{0,1},{1,0},{2,3},{3,2},{4,5},{5,4},{6,7},{7,6},{8,9},{9,8},{10,11... | collective-permute-start | bytes 196616 | tf_op jit(solution)/shard_map/ppermute | solution.py:281
  76.9 2.5 %collective-permute-start.36 = (bf16[32,1024]{1,0:T(8,128)(2,1)S(1)}, bf16[32,1024]{1,0:T(8,128)(2,1)S(1)}, u32[]{:S(2)}, u32[]{:S(2)}) collective-permute-start(bf16[32,1024]{1,0:T(8,128)(2,1)S(1)} %collective-permute-done.35.refs_6_), channel_id=1, source_target_pairs={{0,1},{1,0},{2,3},{3,2},{4,5},{5,4},{6,7},{7,6},{8,9},{9,8},{10,11... | collective-permute-start | bytes 196616 | tf_op jit(solution)/shard_map/ppermute | solution.py:281
  79.3 1.3 %collective-permute-start.44 = (bf16[32,1024]{1,0:T(8,128)(2,1)S(1)}, bf16[32,1024]{1,0:T(8,128)(2,1)S(1)}, u32[]{:S(2)}, u32[]{:S(2)}) collective-permute-start(bf16[32,1024]{1,0:T(8,128)(2,1)S(1)} %collective-permute-done.43.refs_14_), channel_id=1, source_target_pairs={{0,1},{1,0},{2,3},{3,2},{4,5},{5,4},{6,7},{7,6},{8,9},{9,8},{10,11... | collective-permute-start | bytes 196616 | tf_op jit(solution)/shard_map/ppermute | solution.py:281
  82.9 1.3 %collective-permute-start.46 = (bf16[32,1024]{1,0:T(8,128)(2,1)S(1)}, bf16[32,1024]{1,0:T(8,128)(2,1)S(1)}, u32[]{:S(2)}, u32[]{:S(2)}) collective-permute-start(bf16[32,1024]{1,0:T(8,128)(2,1)S(1)} %get-tuple-element.57), channel_id=1, source_target_pairs={{0,1},{1,0},{2,3},{3,2},{4,5},{5,4},{6,7},{7,6},{8,9},{9,8},{10,11... | collective-permute-start | bytes 196616 | tf_op jit(solution)/shard_map/ppermute | solution.py:281
  83.1 18.8 %collective-permute-start.45 = (bf16[32,1024]{1,0:T(8,128)(2,1)S(1)}, bf16[32,1024]{1,0:T(8,128)(2,1)S(1)}, u32[]{:S(2)}, u32[]{:S(2)}) collective-permute-start(bf16[32,1024]{1,0:T(8,128)(2,1)S(1)} %get-tuple-element.55), channel_id=1, source_target_pairs={{0,1},{1,0},{2,3},{3,2},{4,5},{5,4},{6,7},{7,6},{8,9},{9,8},{10,11... | collective-permute-start | bytes 196616 | tf_op jit(solution)/shard_map/ppermute | solution.py:281
  83.5 9.2 %collective-permute-start.48 = (bf16[32,1024]{1,0:T(8,128)(2,1)S(1)}, bf16[32,1024]{1,0:T(8,128)(2,1)S(1)}, u32[]{:S(2)}, u32[]{:S(2)}) collective-permute-start(bf16[32,1024]{1,0:T(8,128)(2,1)S(1)} %get-tuple-element.59), channel_id=1, source_target_pairs={{0,1},{1,0},{2,3},{3,2},{4,5},{5,4},{6,7},{7,6},{8,9},{9,8},{10,11... | collective-permute-start | bytes 196616 | tf_op jit(solution)/shard_map/ppermute | solution.py:281
  83.6 1.3 %collective-permute-start.49 = (bf16[32,1024]{1,0:T(8,128)(2,1)S(1)}, bf16[32,1024]{1,0:T(8,128)(2,1)S(1)}, u32[]{:S(2)}, u32[]{:S(2)}) collective-permute-start(bf16[32,1024]{1,0:T(8,128)(2,1)S(1)} %get-tuple-element.61), channel_id=1, source_target_pairs={{0,1},{1,0},{2,3},{3,2},{4,5},{5,4},{6,7},{7,6},{8,9},{9,8},{10,11... | collective-permute-start | bytes 196616 | tf_op jit(solution)/shard_map/ppermute | solution.py:281
  84.0 12.4 %collective-permute-start.52 = (bf16[32,1024]{1,0:T(8,128)(2,1)S(1)}, bf16[32,1024]{1,0:T(8,128)(2,1)S(1)}, u32[]{:S(2)}, u32[]{:S(2)}) collective-permute-start(bf16[32,1024]{1,0:T(8,128)(2,1)S(1)} %get-tuple-element.63), channel_id=1, source_target_pairs={{0,1},{1,0},{2,3},{3,2},{4,5},{5,4},{6,7},{7,6},{8,9},{9,8},{10,11... | collective-permute-start | bytes 196616 | tf_op jit(solution)/shard_map/ppermute | solution.py:281
  84.2 2.3 %collective-permute-start.53 = (bf16[32,1024]{1,0:T(8,128)(2,1)S(1)}, bf16[32,1024]{1,0:T(8,128)(2,1)S(1)}, u32[]{:S(2)}, u32[]{:S(2)}) collective-permute-start(bf16[32,1024]{1,0:T(8,128)(2,1)S(1)} %get-tuple-element.65), channel_id=1, source_target_pairs={{0,1},{1,0},{2,3},{3,2},{4,5},{5,4},{6,7},{7,6},{8,9},{9,8},{10,11... | collective-permute-start | bytes 196616 | tf_op jit(solution)/shard_map/ppermute | solution.py:281
  84.9 1.3 %collective-permute-start.56 = (bf16[32,1024]{1,0:T(8,128)(2,1)S(1)}, bf16[32,1024]{1,0:T(8,128)(2,1)S(1)}, u32[]{:S(2)}, u32[]{:S(2)}) collective-permute-start(bf16[32,1024]{1,0:T(8,128)(2,1)S(1)} %get-tuple-element.69), channel_id=1, source_target_pairs={{0,1},{1,0},{2,3},{3,2},{4,5},{5,4},{6,7},{7,6},{8,9},{9,8},{10,11... | collective-permute-start | bytes 196616 | tf_op jit(solution)/shard_map/ppermute | solution.py:281
  86.2 1.8 %collective-permute-start.55 = (bf16[32,1024]{1,0:T(8,128)(2,1)S(1)}, bf16[32,1024]{1,0:T(8,128)(2,1)S(1)}, u32[]{:S(2)}, u32[]{:S(2)}) collective-permute-start(bf16[32,1024]{1,0:T(8,128)(2,1)S(1)} %get-tuple-element.67), channel_id=1, source_target_pairs={{0,1},{1,0},{2,3},{3,2},{4,5},{5,4},{6,7},{7,6},{8,9},{9,8},{10,11... | collective-permute-start | bytes 196616 | tf_op jit(solution)/shard_map/ppermute | solution.py:281
  86.6 4.7 %collective-permute-start.57 = (bf16[32,1024]{1,0:T(8,128)(2,1)S(1)}, bf16[32,1024]{1,0:T(8,128)(2,1)S(1)}, u32[]{:S(2)}, u32[]{:S(2)}) collective-permute-start(bf16[32,1024]{1,0:T(8,128)(2,1)S(1)} %add_convert_fusion.10), channel_id=1, source_target_pairs={{0,2},{1,3},{2,0},{3,1},{4,6},{5,7},{6,4},{7,5},{8,10},{9,11},{10,... | collective-permute-start | bytes 196616 | tf_op jit(solution)/shard_map/ppermute | solution.py:281
  88.0 13.9 %collective-permute-start.47 = (bf16[32,1024]{1,0:T(8,128)(2,1)S(1)}, bf16[32,1024]{1,0:T(8,128)(2,1)S(1)}, u32[]{:S(2)}, u32[]{:S(2)}) collective-permute-start(bf16[32,1024]{1,0:T(8,128)(2,1)S(1)} %add_convert_fusion.14), channel_id=1, source_target_pairs={{0,2},{1,3},{2,0},{3,1},{4,6},{5,7},{6,4},{7,5},{8,10},{9,11},{10,... | collective-permute-start | bytes 196616 | tf_op jit(solution)/shard_map/ppermute | solution.py:281
  91.3 4.3 %collective-permute-start.50 = (bf16[32,1024]{1,0:T(8,128)(2,1)S(1)}, bf16[32,1024]{1,0:T(8,128)(2,1)S(1)}, u32[]{:S(2)}, u32[]{:S(2)}) collective-permute-start(bf16[32,1024]{1,0:T(8,128)(2,1)S(1)} %add_convert_fusion.13), channel_id=1, source_target_pairs={{0,2},{1,3},{2,0},{3,1},{4,6},{5,7},{6,4},{7,5},{8,10},{9,11},{10,... | collective-permute-start | bytes 196616 | tf_op jit(solution)/shard_map/ppermute | solution.py:281
  92.8 4.9 %collective-permute-start.54 = (bf16[32,1024]{1,0:T(8,128)(2,1)S(1)}, bf16[32,1024]{1,0:T(8,128)(2,1)S(1)}, u32[]{:S(2)}, u32[]{:S(2)}) collective-permute-start(bf16[32,1024]{1,0:T(8,128)(2,1)S(1)} %add_convert_fusion.11), channel_id=1, source_target_pairs={{0,2},{1,3},{2,0},{3,1},{4,6},{5,7},{6,4},{7,5},{8,10},{9,11},{10,... | collective-permute-start | bytes 196616 | tf_op jit(solution)/shard_map/ppermute | solution.py:281
  95.5 4.3 %collective-permute-start.58 = (bf16[32,1024]{1,0:T(8,128)(2,1)S(1)}, bf16[32,1024]{1,0:T(8,128)(2,1)S(1)}, u32[]{:S(2)}, u32[]{:S(2)}) collective-permute-start(bf16[32,1024]{1,0:T(8,128)(2,1)S(1)} %add_convert_fusion.9), channel_id=1, source_target_pairs={{0,4},{1,5},{2,6},{3,7},{4,0},{5,1},{6,2},{7,3},{8,12},{9,13},{10,... | collective-permute-start | bytes 196616 | tf_op jit(solution)/shard_map/ppermute | solution.py:281
  96.4 5.5 %collective-permute-start.51 = (bf16[32,1024]{1,0:T(8,128)(2,1)S(1)}, bf16[32,1024]{1,0:T(8,128)(2,1)S(1)}, u32[]{:S(2)}, u32[]{:S(2)}) collective-permute-start(bf16[32,1024]{1,0:T(8,128)(2,1)S(1)} %add_convert_fusion.12), channel_id=1, source_target_pairs={{0,4},{1,5},{2,6},{3,7},{4,0},{5,1},{6,2},{7,3},{8,12},{9,13},{10,... | collective-permute-start | bytes 196616 | tf_op jit(solution)/shard_map/ppermute | solution.py:281
  99.8 5.9 %collective-permute-start.59 = (bf16[32,1024]{1,0:T(8,128)(2,1)S(1)}, bf16[32,1024]{1,0:T(8,128)(2,1)S(1)}, u32[]{:S(2)}, u32[]{:S(2)}) collective-permute-start(bf16[32,1024]{1,0:T(8,128)(2,1)S(1)} %add_convert_fusion.8), channel_id=1, source_target_pairs={{0,8},{1,9},{2,10},{3,11},{4,12},{5,13},{6,14},{7,15},{8,0},{9,1},... | collective-permute-start | bytes 196616 | tf_op jit(solution)/shard_map/ppermute | solution.py:281
  (9 other events, 42.1 us)
